TPU v7x, 128 devices: a whole 4x4x4 slice. The times are simulated.
128 devices in a mesh: ep: 32 (over y, x, core), dp: 4 (over z).
Axes of the slice: x: 4, y: 4, z: 4, core: 2. Of those that a mesh axis runs over, the one named last changes fastest.
Arguments:
- resid: bfloat16 [2048, 4096], P(('ep', 'dp')), may hold values from -6 to 6
- queries: bfloat16 [2048, 8192], P(('ep', 'dp')), may hold values from -4.5 to 4.5
- new_keys: bfloat16 [2048, 512], P(('ep', 'dp')), may hold values from -4.5 to 4.5
- new_values: bfloat16 [2048, 512], P(('ep', 'dp')), may hold values from -6 to 6
- cache_keys: bfloat16 [2048, 128, 512], P(('ep', 'dp')), may hold values from -4.5 to 4.5
- cache_values: bfloat16 [2048, 128, 512], P(('ep', 'dp')), may hold values from -6 to 6
- cache_len: int32 [2048], P(('ep', 'dp')), may hold values from 1 to 128
- out_proj: bfloat16 [8192, 4096], P('ep'), may hold values from -0.0625 to 0.0625
- norm_gain: float32 [4096], replicated, may hold values from 0.1 to 1.9
- router: bfloat16 [4096, 64], replicated, may hold values from -4 to 4
- expert_ids: int32 [2048, 8], P(('ep', 'dp')), may hold values from 0 to 63, all different within a row; in each aligned block of 16 rows (0 to 15, 16 to 31, ...) at most 4 rows name the same one
- gate_slab: bfloat16 [128, 4096, 384], P(('ep', 'dp')), may hold values from -0.09375 to 0.09375
- up_slab: bfloat16 [128, 4096, 384], P(('ep', 'dp')), may hold values from -0.09375 to 0.09375
- down_slab: bfloat16 [128, 384, 4096], P(('ep', 'dp')), may hold values from -0.21875 to 0.21875
Outputs:
- mixed: float32 [2048, 4096], P(('ep', 'dp'))
Inputs may be any that keep to these rules, and one draw needn't show every extreme that they name: `expert_ids`: each row names 8 different experts; among the rows of one device no expert is named by more than 4 rows.
All inputs are finite; a program needn't handle non-finite values.
Results may differ from a plain program's by a relative error of at most 0.009.
Values may be sent and summed in bfloat16 or wider, within the bound.
A program may use at most 128 MiB of HBM per device.

v0:
```python
import math

import jax
import jax.numpy as jnp
from jax import lax
from jax.sharding import PartitionSpec as P

D = 4096
H = 64
KVH = 4
HD = 128
TOP = 8


def from_partner(value, axis, distance):
    mask = 2**distance
    pairs = [(source, source ^ mask) for source in range(lax.axis_size(axis))]
    return lax.ppermute(value, axis, pairs)


def attend(queries, new_keys, new_values, cache_keys, cache_values, cache_len):
    local_rows = queries.shape[0]
    cache_span = cache_keys.shape[1]
    group_size = H // KVH
    query_heads = queries.reshape(local_rows, KVH, group_size, HD)
    past_keys = cache_keys.reshape(local_rows, cache_span, KVH, HD)
    past_values = cache_values.reshape(local_rows, cache_span, KVH, HD)
    score_scale = 1.0 / math.sqrt(HD)
    past_scores = (
        jnp.einsum("tgqd,tcgd->tgqc", query_heads, past_keys, preferred_element_type=jnp.float32)
        * score_scale
    )
    own_scores = (
        jnp.einsum(
            "tgqd,tgd->tgq",
            query_heads,
            new_keys.reshape(local_rows, KVH, HD),
            preferred_element_type=jnp.float32,
        )
        * score_scale
    )
    is_valid = lax.broadcasted_iota(jnp.int32, (local_rows, cache_span), 1) < cache_len[:, None]
    past_scores = jnp.where(is_valid[:, None, None, :], past_scores, -1e30)
    peak_score = jnp.maximum(jnp.max(past_scores, axis=3), own_scores)
    past_exp = jnp.exp(past_scores - peak_score[..., None])
    own_exp = jnp.exp(own_scores - peak_score)
    denom_sum = jnp.sum(past_exp, axis=3) + own_exp
    past_weights = (past_exp / denom_sum[..., None]).astype(jnp.bfloat16)
    own_weights = (own_exp / denom_sum).astype(jnp.bfloat16)
    blended = jnp.einsum(
        "tgqc,tcgd->tgqd", past_weights, past_values, preferred_element_type=jnp.float32
    )
    blended = blended + own_weights.astype(jnp.float32)[..., None] * new_values.reshape(
        local_rows, KVH, 1, HD
    ).astype(jnp.float32)
    return blended.reshape(local_rows, H * HD).astype(jnp.bfloat16)


def expert_ffn(rows_in, gate_part, up_part, down_part):
    gate_val = jnp.dot(rows_in, gate_part, preferred_element_type=jnp.float32)
    up_val = jnp.dot(rows_in, up_part, preferred_element_type=jnp.float32)
    activated = (jax.nn.silu(gate_val) * up_val).astype(jnp.bfloat16)
    return jnp.dot(activated, down_part, preferred_element_type=jnp.float32)


def local(
    resid,
    queries,
    new_keys,
    new_values,
    cache_keys,
    cache_values,
    cache_len,
    out_proj,
    norm_gain,
    router,
    expert_ids,
    gate_slab,
    up_slab,
    down_slab,
):
    local_rows = resid.shape[0]
    attended = attend(queries, new_keys, new_values, cache_keys, cache_values, cache_len)
    regrouped = lax.all_to_all(attended, "ep", split_axis=1, concat_axis=0, tiled=True)
    attn_out = lax.psum_scatter(
        jnp.dot(regrouped, out_proj, preferred_element_type=jnp.float32).astype(jnp.bfloat16),
        "ep",
        scatter_dimension=0,
        tiled=True,
    ).astype(jnp.float32)
    hidden = resid.astype(jnp.float32) + attn_out
    meansq = jnp.mean(hidden * hidden, axis=1, keepdims=True)
    normed = (hidden * lax.rsqrt(jnp.maximum(meansq, 0.25)) * norm_gain).astype(jnp.bfloat16)
    logits = jnp.dot(normed, router, preferred_element_type=jnp.float32)
    experts = router.shape[1]
    labels = jnp.arange(experts, dtype=jnp.int32)
    onehot = expert_ids[:, :, None] == labels[None, None, :]
    chosen = jnp.sum(jnp.where(onehot, logits[:, None, :], 0.0), axis=2)
    peak_logit = jnp.max(chosen, axis=1, keepdims=True)
    exp_logit = jnp.exp(chosen - peak_logit)
    gate_probs = (exp_logit / jnp.sum(exp_logit, axis=1, keepdims=True)).astype(jnp.bfloat16)
    per_token = jnp.sum(onehot.astype(jnp.int32), axis=1)
    before = jnp.cumsum(per_token, axis=0) - per_token
    ranking = jnp.sum(jnp.where(onehot, before[:, None, :], 0), axis=2)
    slab_count = lax.axis_size("ep") * lax.axis_size("dp")
    half_slots = (4 * local_rows * TOP + 5 * experts - 1) // (5 * experts)
    target = (2 * expert_ids + ranking % 2) * half_slots + ranking // 2
    places = jnp.arange(slab_count * half_slots, dtype=jnp.int32)
    slot_match = target[:, :, None] == places[None, None, :]
    dispatch = jnp.any(slot_match, axis=1).astype(jnp.bfloat16)
    combine = jnp.sum(
        jnp.where(slot_match, gate_probs.astype(jnp.float32)[:, :, None], 0.0), axis=1
    ).astype(jnp.bfloat16)
    outgoing = lax.dot_general(
        dispatch, normed, (((0,), (0,)), ((), ())), preferred_element_type=jnp.float32
    )
    outgoing = outgoing.astype(jnp.bfloat16).reshape(slab_count, half_slots, D)
    partner = from_partner((gate_slab, up_slab, down_slab), "dp", 0)
    incoming = lax.all_to_all(outgoing, ("ep", "dp"), split_axis=0, concat_axis=0, tiled=True)
    sources, slot_count, feature_dim = incoming.shape
    flat_rows = incoming.reshape(sources * slot_count, feature_dim)
    produced = expert_ffn(flat_rows, gate_slab[0], up_slab[0], down_slab[0])
    produced = produced + expert_ffn(flat_rows, partner[0][0], partner[1][0], partner[2][0])
    returned = lax.all_to_all(
        produced.astype(jnp.bfloat16).reshape(sources, slot_count, feature_dim),
        ("ep", "dp"),
        split_axis=0,
        concat_axis=0,
        tiled=True,
    )
    expert_mix = jnp.dot(
        combine, returned.reshape(slab_count * half_slots, D), preferred_element_type=jnp.float32
    )
    return hidden + expert_mix


def solution(mesh):
    in_specs = (
        P(("ep", "dp"), None),
        P(("ep", "dp"), None),
        P(("ep", "dp"), None),
        P(("ep", "dp"), None),
        P(("ep", "dp"), None, None),
        P(("ep", "dp"), None, None),
        P(("ep", "dp")),
        P("ep", None),
        P(),
        P(),
        P(("ep", "dp"), None),
        P(("ep", "dp"), None, None),
        P(("ep", "dp"), None, None),
        P(("ep", "dp"), None, None),
    )
    out_specs = P(("ep", "dp"), None)
    return jax.shard_map(local, mesh=mesh, in_specs=in_specs, out_specs=out_specs, check_vma=False)
```

profile of v0, /device:TPU:1, one launch (start us, length us, event | category | flops | bytes accessed | tf_op | source)
XLA Modules:
  0.0 358.3 jit_solution(8555865213800240710)
XLA Ops:
  6.5 0.9 iota_compare_fusion.2
  7.4 0.7 reshape.128
  8.1 0.7 reshape.124
  8.9 1.0 copy.44
  10.1 3.0 fusion.68
  13.2 0.4 fusion.38
  13.7 0.8 fusion.27
  14.7 17.3 %all_to_all.26 = bf16[16,32,256]{2,0,1:T(8,128)(2,1)S(1)} all-to-all(bf16[16,32,256]{2,0,1:T(8,128)(2,1)S(1)} %copy.33), channel_id=1, replica_groups=mesh['ep'=32,'dp'=4] {'ep'}, dimensions={1} | all-to-all | bytes 524288 | tf_op jit(solution)/shard_map/all_to_all | solution.py:84
  32.0 3.2 convolution_convert_fusion
  35.2 1.7 collective-permute-start.1
  37.1 0.4 select_reduce_fusion.2
  37.7 76.6 %reduce-scatter.2.cloned.1.call-done = bf16[16,4096]{1,0:T(8,128)(2,1)} async-done(((bf16[512,4096]{1,0:T(8,128)(2,1)}), bf16[16,4096]{1,0:T(8,128)(2,1)}) %reduce-scatter.2.cloned.1.call-update) | async-done | bytes 131088 | tf_op jit(solution)/shard_map/reduce_scatter | solution.py:85
  114.2 1.1 multiply_reduce_fusion
  115.3 3.0 convolution_convert_fusion.1
  118.3 4.4 %reshape.120 = bf16[128,2,4096]{2,1,0:T(2,128)(2,1)} reshape(bf16[256,4096]{1,0:T(8,128)(2,1)} %convolution_convert_fusion.1) | data formatting | bytes 4194304 | tf_op jit(solution)/shard_map/reshape | solution.py:117
  122.7 9.9 %all-to-all-start.1 = ((bf16[128,2,4096]{2,1,0:T(2,128)(2,1)}), bf16[128,2,4096]{2,1,0:T(2,128)(2,1)}, u32[]{:S(2)}, u32[]{:S(2)}) async-start(bf16[128,2,4096]{2,1,0:T(2,128)(2,1)} %reshape.120), calls=%async_computation.2 | async-start | bytes 4194304 | tf_op jit(solution)/shard_map/all_to_all | solution.py:119
  132.6 1.6 collective-permute-start
  134.2 0.3 collective-permute-start.2
  134.5 28.3 %all-to-all-done.1 = bf16[128,2,4096]{2,1,0:T(2,128)(2,1)} async-done(((bf16[128,2,4096]{2,1,0:T(2,128)(2,1)}), bf16[128,2,4096]{2,1,0:T(2,128)(2,1)}, u32[]{:S(2)}, u32[]{:S(2)}) %all-to-all-start.1) | async-done | bytes 2097184 | tf_op jit(solution)/shard_map/all_to_all | solution.py:119
  162.8 4.1 %reshape.121 = bf16[256,4096]{1,0:T(8,128)(2,1)} reshape(bf16[128,2,4096]{2,1,0:T(2,128)(2,1)} %all-to-all-done.1) | data formatting | bytes 4194304 | tf_op jit(solution)/shard_map/reshape | solution.py:121
  166.9 3.9 %fusion.10 = f32[256,384]{1,0:T(8,128)S(1)} fusion(bf16[256,4096]{1,0:T(8,128)(2,1)} %reshape.121, bf16[1,4096,384]{2,1,0:T(8,128)(2,1)} %param.25), kind=kOutput, calls=%fused_computation.14 | convolution fusion | flops 805306368 | bytes 5636096 | tf_op jit(solution)/shard_map/dot_general | solution.py:60
  170.8 3.2 fusion.2
  174.0 7.8 %fusion.6 = f32[256,4096]{1,0:T(8,128)} fusion(bf16[1,384,4096]{2,1,0:T(8,128)(2,1)} %param.27, bf16[256,4096]{1,0:T(8,128)(2,1)} %reshape.121, bf16[1,4096,384]{2,1,0:T(8,128)(2,1)} %param.26, f32[256,384]{1,0:T(8,128)S(1)} %fusion.10), kind=kOutput, calls=%fused_computation.10 | convolution fusion | flops 1611202560 | bytes 12976128 | tf_op jit(solution)/shard_map/dot_general | solution.py:63
  181.9 42.3 %collective-permute-done = bf16[1,4096,384]{2,1,0:T(8,128)(2,1)} collective-permute-done((bf16[1,4096,384]{2,1,0:T(8,128)(2,1)}, bf16[1,4096,384]{2,1,0:T(8,128)(2,1)}, u32[]{:S(2)}, u32[]{:S(2)}) %collective-permute-start) | collective-permute-done | bytes 3145760 | tf_op jit(solution)/shard_map/ppermute | solution.py:18
  224.2 67.4 %collective-permute-done.2 = bf16[1,384,4096]{2,1,0:T(8,128)(2,1)} collective-permute-done((bf16[1,384,4096]{2,1,0:T(8,128)(2,1)}, bf16[1,384,4096]{2,1,0:T(8,128)(2,1)}, u32[]{:S(2)}, u32[]{:S(2)}) %collective-permute-start.2) | collective-permute-done | bytes 3145760 | tf_op jit(solution)/shard_map/ppermute | solution.py:18
  291.6 8.5 %fusion = bf16[256,4096]{1,0:T(8,128)(2,1)} fusion(f32[256,4096]{1,0:T(8,128)} %fusion.6, bf16[1,384,4096]{2,1,0:T(8,128)(2,1)} %collective-permute-done.2, f32[256,384]{1,0:T(8,128)S(1)} %fusion.2, bf16[256,4096]{1,0:T(8,128)(2,1)} %reshape.121, bf16[1,4096,384]{2,1,0:T(8,128)(2,1)} %collective-permute-done), kind=kOutput, calls=%fused_computation.2 | convolution fusion | flops 1613299712 | bytes 15073280 | tf_op jit(solution)/shard_map/dot_general | solution.py:63
  300.0 4.4 %reshape.122 = bf16[128,2,4096]{2,1,0:T(2,128)(2,1)} reshape(bf16[256,4096]{1,0:T(8,128)(2,1)} %fusion) | data formatting | bytes 4194304 | tf_op jit(solution)/shard_map/reshape | solution.py:125
  304.5 10.0 %all-to-all-start.2 = ((bf16[128,2,4096]{2,1,0:T(2,128)(2,1)}), bf16[128,2,4096]{2,1,0:T(2,128)(2,1)}, u32[]{:S(2)}, u32[]{:S(2)}) async-start(bf16[128,2,4096]{2,1,0:T(2,128)(2,1)} %reshape.122), calls=%async_computation.3 | async-start | bytes 4194304 | tf_op jit(solution)/shard_map/all_to_all | solution.py:124
  314.5 0.3 fusion.67
  315.4 29.2 %all-to-all-done.2 = bf16[128,2,4096]{2,1,0:T(2,128)(2,1)} async-done(((bf16[128,2,4096]{2,1,0:T(2,128)(2,1)}), bf16[128,2,4096]{2,1,0:T(2,128)(2,1)}, u32[]{:S(2)}, u32[]{:S(2)}) %all-to-all-start.2) | async-done | bytes 2097184 | tf_op jit(solution)/shard_map/all_to_all | solution.py:124
  344.6 4.1 %reshape.123 = bf16[256,4096]{1,0:T(8,128)(2,1)} reshape(bf16[128,2,4096]{2,1,0:T(2,128)(2,1)} %all-to-all-done.2) | data formatting | bytes 4194304 | tf_op jit(solution)/shard_map/reshape | solution.py:132
  348.8 2.7 convolution_add_fusion.1
  (38 shorter events, 1.6 us)
Async XLA Ops:
  6.5 25.4 %copy-start = (bf16[256,4096]{1,0:T(8,128)(2,1)S(1)}, bf16[256,4096]{1,0:T(8,128)(2,1)}, u32[]{:S(2)}) copy-start(bf16[256,4096]{1,0:T(8,128)(2,1)} %param.21) | copy-start | bytes 6291460
  6.5 107.7 %reduce-scatter.2.cloned.1.call-start = ((), (), s32[]{:S(2)}) async-start(), calls=%async_computation.4 | async-start | bytes 4325376 | tf_op jit(solution)/shard_map/reduce_scatter | solution.py:85
  9.9 3.8 %copy-start.7 = (bf16[16,128,512]{2,1,0:T(8,128)(2,1)S(1)}, bf16[16,128,512]{2,1,0:T(8,128)(2,1)}, u32[]{:S(2)}) copy-start(bf16[16,128,512]{2,1,0:T(8,128)(2,1)} %param.19) | copy-start | bytes 6291460
  35.1 1.8 copy-start.6
  35.1 79.1 %copy-start.2 = (bf16[16,4096]{1,0:T(8,128)(2,1)S(1)}, bf16[16,4096]{1,0:T(8,128)(2,1)}, u32[]{:S(2)}) copy-start(bf16[16,4096]{1,0:T(8,128)(2,1)} %param.14) | copy-start | bytes 393220
  35.1 80.2 %copy-start.5 = (f32[4096]{0:T(1024)S(1)}, f32[4096]{0:T(1024)}, u32[]{:S(2)}) copy-start(f32[4096]{0:T(1024)} %param.22) | copy-start | bytes 49156
  35.2 135.7 %collective-permute-start.1 = (bf16[1,4096,384]{2,1,0:T(8,128)(2,1)}, bf16[1,4096,384]{2,1,0:T(8,128)(2,1)}, u32[]{:S(2)}, u32[]{:S(2)}) collective-permute-start(bf16[1,4096,384]{2,1,0:T(8,128)(2,1)} %param.26), channel_id=1, source_target_pairs={{0,1},{1,0},{2,3},{3,2},{4,5},{5,4},{6,7},{7,6},{8,9},{9,8},{10,11... | collective-permute-start | bytes 9437192 | tf_op jit(solution)/shard_map/ppermute | solution.py:18
  122.7 40.1 %all-to-all-start.1 = ((bf16[128,2,4096]{2,1,0:T(2,128)(2,1)}), bf16[128,2,4096]{2,1,0:T(2,128)(2,1)}, u32[]{:S(2)}, u32[]{:S(2)}) async-start(bf16[128,2,4096]{2,1,0:T(2,128)(2,1)} %reshape.120), calls=%async_computation.2 | async-start | bytes 4194304 | tf_op jit(solution)/shard_map/all_to_all | solution.py:119
  132.6 91.5 %collective-permute-start = (bf16[1,4096,384]{2,1,0:T(8,128)(2,1)}, bf16[1,4096,384]{2,1,0:T(8,128)(2,1)}, u32[]{:S(2)}, u32[]{:S(2)}) collective-permute-start(bf16[1,4096,384]{2,1,0:T(8,128)(2,1)} %param.25), channel_id=1, source_target_pairs={{0,1},{1,0},{2,3},{3,2},{4,5},{5,4},{6,7},{7,6},{8,9},{9,8},{10,11... | collective-permute-start | bytes 9437192 | tf_op jit(solution)/shard_map/ppermute | solution.py:18
  134.2 157.4 %collective-permute-start.2 = (bf16[1,384,4096]{2,1,0:T(8,128)(2,1)}, bf16[1,384,4096]{2,1,0:T(8,128)(2,1)}, u32[]{:S(2)}, u32[]{:S(2)}) collective-permute-start(bf16[1,384,4096]{2,1,0:T(8,128)(2,1)} %param.27), channel_id=1, source_target_pairs={{0,1},{1,0},{2,3},{3,2},{4,5},{5,4},{6,7},{7,6},{8,9},{9,8},{10,11... | collective-permute-start | bytes 9437192 | tf_op jit(solution)/shard_map/ppermute | solution.py:18
  166.9 3.9 %copy-start.1 = (bf16[256,4096]{1,0:T(8,128)(2,1)S(1)}, bf16[256,4096]{1,0:T(8,128)(2,1)}, u32[]{:S(2)}) copy-start(bf16[256,4096]{1,0:T(8,128)(2,1)} %reshape.121) | copy-start | bytes 6291460
  304.4 10.0 %copy-start.3 = (bf16[16,4096]{1,0:T(8,128)(2,1)S(1)}, bf16[16,4096]{1,0:T(8,128)(2,1)}, u32[]{:S(2)}) copy-start(bf16[16,4096]{1,0:T(8,128)(2,1)} %reduce-scatter.2.cloned.1.call-done) | copy-start | bytes 393220
  304.5 10.0 %copy-start.4 = (bf16[4096,64]{0,1:T(8,128)(2,1)S(1)}, bf16[4096,64]{0,1:T(8,128)(2,1)}, u32[]{:S(2)}) copy-start(bf16[4096,64]{0,1:T(8,128)(2,1)} %param.23) | copy-start | bytes 1572868
  304.5 40.2 %all-to-all-start.2 = ((bf16[128,2,4096]{2,1,0:T(2,128)(2,1)}), bf16[128,2,4096]{2,1,0:T(2,128)(2,1)}, u32[]{:S(2)}, u32[]{:S(2)}) async-start(bf16[128,2,4096]{2,1,0:T(2,128)(2,1)} %reshape.122), calls=%async_computation.3 | async-start | bytes 4194304 | tf_op jit(solution)/shard_map/all_to_all | solution.py:124
Sparse Core Ops, SparseCore 0:
  35.3 78.8 reduce-scatter.1
where the time goes:
time: 359 us; the launch traced here: 358 us
  waiting for transfers between devices  244 us (68%)
  matrix products  36.6 us (10%)
  starting transfers between devices  23.4 us (7%)
  local copies, waits for them, and re-layouts  20 us (6%)
  blocking collectives  17.3 us (5%)
  between operations  13.6 us (4%)
    ppermute x3, waiting for transfers between devices, from_partner(): return lax.ppermute(value, axis, pairs)  110 us
    reduce_scatter x1, waiting for transfers between devices, local(): lax.psum_scatter(jnp.dot(regrouped, out_proj, preferred_element_type=jnp....  76.6 us
    all_to_all x1, waiting for transfers between devices, local(): lax.all_to_all(produced.astype(jnp.bfloat16).reshape(sources, slot_count,...  29.2 us
    all_to_all x1, waiting for transfers between devices, local(): lax.all_to_all(outgoing, ('ep', 'dp'), split_axis=0, concat_axis=0, tiled...  28.3 us
    all_to_all x1, blocking collectives, local(): lax.all_to_all(attended, 'ep', split_axis=1, concat_axis=0, tiled=True)  17.3 us
    dot_general x2, matrix products, expert_ffn(): return jnp.dot(activated, down_part, preferred_element_type=jnp.float32)  16.3 us
    all_to_all x1, starting transfers between devices, local(): lax.all_to_all(produced.astype(jnp.bfloat16).reshape(sources, slot_count,...  10 us
    all_to_all x1, starting transfers between devices, local(): lax.all_to_all(outgoing, ('ep', 'dp'), split_axis=0, concat_axis=0, tiled...  9.87 us
  transfers between devices with their start and end apart: 6, of which 5 were waited for; matrix products, arithmetic and copies ran while one was open for 8% of the time, Pallas kernels for 0%

commit v1 on v0

--- a/solution.py
+++ b/solution.py
@@ -1,8 +1,11 @@
+import functools
 import math
 
 import jax
 import jax.numpy as jnp
 from jax import lax
+from jax.experimental import pallas as pl
+from jax.experimental.pallas import tpu as pltpu
 from jax.sharding import PartitionSpec as P
 
 D = 4096
@@ -10,12 +13,11 @@
 KVH = 4
 HD = 128
 TOP = 8
-
-
-def from_partner(value, axis, distance):
-    mask = 2**distance
-    pairs = [(source, source ^ mask) for source in range(lax.axis_size(axis))]
-    return lax.ppermute(value, axis, pairs)
+MESH = pl.DeviceIdType.MESH
+
+PART = 1408
+ORDER = (("x", "y", "z"), ("y", "z", "x"), ("z", "x", "y"))
+HF = 384
 
 
 def attend(queries, new_keys, new_values, cache_keys, cache_values, cache_len):
@@ -56,11 +58,414 @@
     return blended.reshape(local_rows, H * HD).astype(jnp.bfloat16)
 
 
-def expert_ffn(rows_in, gate_part, up_part, down_part):
-    gate_val = jnp.dot(rows_in, gate_part, preferred_element_type=jnp.float32)
-    up_val = jnp.dot(rows_in, up_part, preferred_element_type=jnp.float32)
-    activated = (jax.nn.silu(gate_val) * up_val).astype(jnp.bfloat16)
-    return jnp.dot(activated, down_part, preferred_element_type=jnp.float32)
+class Place:
+    def __init__(self):
+        ep = lax.axis_index("ep")
+        self.c = lax.rem(ep, 2)
+        self.coord = {
+            "x": lax.rem(lax.div(ep, 2), 4),
+            "y": lax.div(ep, 8),
+            "z": lax.axis_index("dp"),
+        }
+
+    def rel(self, dim, offset):
+        if isinstance(offset, int) and offset == 0:
+            return self.coord[dim]
+        return lax.rem(self.coord[dim] + offset, 4)
+
+    def device(self, dim=None, offset=0, other_core=False):
+        at = dict(self.coord)
+        if dim is not None:
+            at[dim] = self.rel(dim, offset)
+        core = 1 - self.c if other_core else self.c
+        return ((at["y"] * 4 + at["x"]) * 2 + core, at["z"])
+
+
+class Names:
+    def __init__(self):
+        self.table = {}
+
+    def __call__(self, *key):
+        return self.table.setdefault(key, len(self.table))
+
+
+SENDS = 260
+
+
+def moe_kernel(
+    x_in, gate, up, down, out,
+    rows, gu, dn, acc, act, part, pair_out, pair_in, ra1, ra2, rb1, rb2, rc1, rc2,
+    send_sem, recv_sem, load_sem,
+):
+    here = Place()
+    c = here.c
+    other = 1 - c
+    rel, device = here.rel, here.device
+    ahead = 1 + 2 * c
+    behind = 3 - 2 * c
+    names = Names()
+    pending = {}
+
+    def send(src, dst, key, dev):
+        i = names(*key)
+        copy = pltpu.make_async_remote_copy(
+            src_ref=src, dst_ref=dst, send_sem=send_sem.at[i], recv_sem=recv_sem.at[i],
+            device_id=dev, device_id_type=MESH,
+        )
+        copy.start()
+        pending[key] = copy
+
+    def landed(dst, key):
+        i = names(*key)
+        pltpu.make_async_remote_copy(
+            src_ref=dst, dst_ref=dst, send_sem=send_sem.at[i], recv_sem=recv_sem.at[i],
+            device_id=device(other_core=True), device_id_type=MESH,
+        ).wait_recv()
+
+    def where(p, o1, o2, o3):
+        at = {d: (slice(None) if o is None else rel(d, o)) for d, o in zip(ORDER[p], (o1, o2, o3))}
+        return at["y"], at["x"], at["z"]
+
+    def block(p, o1, o2, o3, core=None):
+        return rows.at[(p, c if core is None else core) + where(p, o1, o2, o3)]
+
+    barrier = pltpu.get_barrier_semaphore()
+    for dim in ("x", "y", "z"):
+        for o in (1, 3):
+            pl.semaphore_signal(barrier, inc=1, device_id=device(dim, o), device_id_type=MESH)
+    pl.semaphore_signal(barrier, inc=1, device_id=device(other_core=True), device_id_type=MESH)
+
+    loads = [
+        pltpu.make_async_copy(gate, gu.at[pl.ds(0, D), pl.ds(0, HF)], load_sem.at[0]),
+        pltpu.make_async_copy(up, gu.at[pl.ds(0, D), pl.ds(HF, HF)], load_sem.at[1]),
+        pltpu.make_async_copy(down, dn.at[:, pl.ds(0, D)], load_sem.at[2]),
+    ]
+    for copy in loads:
+        copy.start()
+    mine = [x_in.at[:, pl.ds(p * PART, PART)] for p in range(3)]
+    for p in range(3):
+        rows[(p, c) + where(p, 0, 0, 0)] = x_in[:, p * PART : (p + 1) * PART]
+    pl.semaphore_wait(barrier, 7)
+
+    parts = range(3)
+    dims = ORDER
+    for p in parts:
+        own = block(p, 0, 0, 0)
+        send(mine[p], own, (p, "1f"), device(dims[p][0], ahead))
+        send(mine[p], own, (p, "1b"), device(dims[p][0], behind))
+    for p in parts:
+        own = block(p, 0, 0, 0)
+        send(mine[p], own, (p, "2+", 0), device(dims[p][1], 1))
+        send(mine[p], own, (p, "2-", 0), device(dims[p][1], 3))
+
+    gu[D:, :] = jnp.zeros((3 * PART - D, 2 * HF), jnp.bfloat16)
+    dn[:, D:] = jnp.zeros((HF, 3 * PART - D), jnp.bfloat16)
+
+    @pl.loop(0, 32)
+    def _(i):
+        acc[i // 16, lax.rem(i, 16) // 4, lax.rem(i, 4)] = jnp.zeros((4, 16, 2 * HF), jnp.float32)
+
+    def send_sub(p, j):
+        ref = block(p, j, 0, 0)
+        send(ref, ref, (p, "2+", j), device(dims[p][1], 1))
+        send(ref, ref, (p, "2-", j), device(dims[p][1], 3))
+
+    def send_line(p, j):
+        ref = block(p, None, j, 0)
+        send(ref, ref, (p, "3+", j), device(dims[p][2], 1))
+        send(ref, ref, (p, "3-", j), device(dims[p][2], 3))
+
+    def pass_on(p, o2, o3):
+        ref = block(p, None, o2, o3)
+        send(ref, ref, (p, "pair", o2, o3), device(other_core=True))
+
+    for p in parts:
+        ref = block(p, behind, 0, 0)
+        landed(ref, (p, "1f"))
+        send(ref, ref, (p, "1g"), device(dims[p][0], ahead))
+        landed(block(p, ahead, 0, 0), (p, "1b"))
+        send_sub(p, 1)
+        send_sub(p, 3)
+    for p in parts:
+        landed(block(p, 2, 0, 0), (p, "1g"))
+        send_sub(p, 2)
+        send_line(p, 0)
+        pass_on(p, 0, 0)
+    for j in (0, 1, 3, 2):
+        for p in parts:
+            ref = block(p, j, 3, 0)
+            landed(ref, (p, "2+", j))
+            if j in (0, 1):
+                send(ref, ref, (p, "2g", j), device(dims[p][1], 1))
+            ref = block(p, j, 1, 0)
+            landed(ref, (p, "2-", j))
+            if j in (3, 2):
+                send(ref, ref, (p, "2g", j), device(dims[p][1], 3))
+    for p in parts:
+        send_line(p, 1)
+        send_line(p, 3)
+        pass_on(p, 1, 0)
+        pass_on(p, 3, 0)
+    for copy in loads:
+        copy.wait()
+    for p in parts:
+        for j in (0, 1, 3, 2):
+            landed(block(p, j, 2, 0), (p, "2g", j))
+        send_line(p, 2)
+        pass_on(p, 2, 0)
+
+    def project(p, o2, o3):
+        landed(block(p, None, o2, o3, other), (p, "pair", o2, o3))
+        at = where(p, None, o2, o3)
+
+        @pl.loop(0, 3)
+        def _(n):
+            cols = pl.ds(pl.multiple_of(n * 256, 256), 256)
+            x = rows[(p, slice(None)) + at].reshape(128, PART)
+            y = jnp.dot(x, gu[p * PART : (p + 1) * PART, cols], preferred_element_type=jnp.float32)
+            idx = (slice(None),) + at + (slice(None), cols)
+            acc[idx] += y.reshape(2, 4, 16, 256)
+
+    seen = None
+    for j in (0, 1, 3, 2):
+        for p in parts:
+            project(p, j, 0)
+        for p in parts:
+            ref = block(p, None, j, 3)
+            landed(ref, (p, "3+", j))
+            if j in (0, 1):
+                send(ref, ref, (p, "3g", j), device(dims[p][2], 1))
+            ref = block(p, None, j, 1)
+            landed(ref, (p, "3-", j))
+            if j in (3, 2):
+                send(ref, ref, (p, "3g", j), device(dims[p][2], 3))
+            pass_on(p, j, 3)
+            pass_on(p, j, 1)
+        if seen is not None:
+            for p in parts:
+                project(p, seen, 3)
+                project(p, seen, 1)
+        seen = j
+    for p in parts:
+        project(p, seen, 3)
+        project(p, seen, 1)
+    for j in (0, 3, 1, 2):
+        for p in parts:
+            landed(block(p, None, j, 2), (p, "3g", j))
+            pass_on(p, j, 2)
+    for j in (0, 3, 1, 2):
+        for p in parts:
+            project(p, j, 2)
+
+    expert = lax.div(lax.axis_index("ep") * 4 + lax.axis_index("dp"), 2)
+
+    @pl.loop(0, 32)
+    def _(i):
+        at = (i // 16, lax.rem(i, 16) // 4, lax.rem(i, 4))
+        sums = acc[at].reshape(64, 2 * HF)
+        tail = rows[(2,) + at + (slice(None), slice(None), slice(PART - 128, PART))]
+        tail = tail.reshape(64, 128).astype(jnp.float32)
+        lanes = lax.broadcasted_iota(jnp.int32, (64, 128), 1)
+        prob = jnp.sum(jnp.where(lanes == expert, tail, 0.0), axis=1, keepdims=True)
+        g, u = sums[:, :HF], sums[:, HF:]
+        h = (g / (1.0 + jnp.exp(-g)) * u).astype(jnp.bfloat16).astype(jnp.float32) * prob
+        act[at] = h.astype(jnp.bfloat16).reshape(4, 16, HF)
+
+    def spot(p, o2, o3):
+        a2 = slice(None) if o2 is None else rel(dims[p][1], o2)
+        a3 = slice(None) if o3 is None else rel(dims[p][0], o3)
+        return (a3, a2) if p == 1 else (a2, a3)
+
+    def line(p, o1, o2):
+        return part.at[(p, o1) + spot(p, o2, None)]
+
+    def sub(p, o3):
+        return part.at[(p, 0) + spot(p, 0, o3)]
+
+    def hidden_of(p, o1, core):
+        at = {d: (rel(d, o1) if d == dims[p][2] else slice(None)) for d in "xyz"}
+        return act[core, at["y"], at["x"], at["z"]].reshape(256, HF)
+
+    def product(p, o1, core, dst):
+        @pl.loop(0, 5)
+        def _(n):
+            cols = pl.ds(pl.multiple_of(n * 256, 256), 256)
+            wcols = pl.ds(pl.multiple_of(p * PART + n * 256, 128), 256)
+            y = jnp.dot(hidden_of(p, o1, core), dn[:, wcols], preferred_element_type=jnp.float32)
+            dst[:, :, :, cols] = y.astype(jnp.bfloat16).reshape(4, 4, 16, 256)
+
+        if p < 2:
+            y = jnp.dot(hidden_of(p, o1, core), dn[:, p * PART + 1280 : (p + 1) * PART], preferred_element_type=jnp.float32)
+            dst[:, :, :, 1280:] = y.astype(jnp.bfloat16).reshape(4, 4, 16, 128)
+        else:
+            dst[:, :, :, 1280:] = jnp.zeros((4, 4, 16, 128), jnp.bfloat16)
+
+    def add(dst, *srcs):
+        @pl.loop(0, 4)
+        def _(i):
+            total = dst[i].astype(jnp.float32)
+            for s in srcs:
+                total += s[i].astype(jnp.float32)
+            dst[i] = total.astype(jnp.bfloat16)
+
+    def add_sub(dst, *srcs):
+        total = dst[...].astype(jnp.float32)
+        for s in srcs:
+            total += s[...].astype(jnp.float32)
+        dst[...] = total.astype(jnp.bfloat16)
+
+    waited = set()
+
+    def sums_for(o1):
+        for p in parts:
+            for key in list(pending):
+                if key[:2] == (p, "sum") and key not in waited:
+                    pending[key].wait_send()
+                    waited.add(key)
+            product(p, o1, other, pair_out.at[p])
+            send(pair_out.at[p], pair_in.at[p, o1], (p, "sum", o1), device(other_core=True))
+        for p in parts:
+            product(p, o1, c, part.at[p, o1])
+        for p in parts:
+            landed(pair_in.at[p, o1], (p, "sum", o1))
+            @pl.loop(0, 4)
+            def _(i):
+                add(part.at[p, o1, i], pair_in.at[p, o1, i])
+
+    def up_of(p, level):
+        return device(dims[p][level], 1)
+
+    def down_of(p, level):
+        return device(dims[p][level], 3)
+
+    UPWARD, DOWNWARD = (2, 1), (3, 0)
+
+    sums_for(2)
+    for k in range(2):
+        for p in parts:
+            send(line(p, 2, UPWARD[k]), ra1.at[p, 0, k], (p, "a1+", k), up_of(p, 2))
+            send(line(p, 2, DOWNWARD[k]), ra1.at[p, 1, k], (p, "a1-", k), down_of(p, 2))
+    sums_for(1)
+    for j in DOWNWARD:
+        for p in parts:
+            send(line(p, 1, j), ra2.at[p, 0, j], (p, "a2+", j), up_of(p, 2))
+    sums_for(3)
+    for j in UPWARD:
+        for p in parts:
+            send(line(p, 3, j), ra2.at[p, 1, j], (p, "a2-", j), down_of(p, 2))
+    for k in range(2):
+        for p in parts:
+            j = UPWARD[k]
+            landed(ra1.at[p, 0, k], (p, "a1+", k))
+            add(line(p, 1, j), ra1.at[p, 0, k])
+            send(line(p, 1, j), ra2.at[p, 0, j], (p, "a2+", j), up_of(p, 2))
+            j = DOWNWARD[k]
+            landed(ra1.at[p, 1, k], (p, "a1-", k))
+            add(line(p, 3, j), ra1.at[p, 1, k])
+            send(line(p, 3, j), ra2.at[p, 1, j], (p, "a2-", j), down_of(p, 2))
+    sums_for(0)
+
+    def finish_line(p, j):
+        landed(ra2.at[p, 0, j], (p, "a2+", j))
+        landed(ra2.at[p, 1, j], (p, "a2-", j))
+        add(line(p, 0, j), ra2.at[p, 0, j], ra2.at[p, 1, j])
+
+    def block_of(p, o2, o3):
+        return part.at[(p, 0) + spot(p, o2, o3)]
+
+    for p in parts:
+        finish_line(p, 2)
+        for k in range(2):
+            send(block_of(p, 2, UPWARD[k]), rb1.at[p, 0, k], (p, "b1+", k), up_of(p, 1))
+            send(block_of(p, 2, DOWNWARD[k]), rb1.at[p, 1, k], (p, "b1-", k), down_of(p, 1))
+    for p in parts:
+        finish_line(p, 3)
+        for j in UPWARD:
+            send(block_of(p, 3, j), rb2.at[p, 1, j], (p, "b2-", j), down_of(p, 1))
+    for p in parts:
+        finish_line(p, 1)
+        for j in DOWNWARD:
+            send(block_of(p, 1, j), rb2.at[p, 0, j], (p, "b2+", j), up_of(p, 1))
+    for k in range(2):
+        for p in parts:
+            j = UPWARD[k]
+            landed(rb1.at[p, 0, k], (p, "b1+", k))
+            add_sub(block_of(p, 1, j), rb1.at[p, 0, k])
+            send(block_of(p, 1, j), rb2.at[p, 0, j], (p, "b2+", j), up_of(p, 1))
+            j = DOWNWARD[k]
+            landed(rb1.at[p, 1, k], (p, "b1-", k))
+            add_sub(block_of(p, 3, j), rb1.at[p, 1, k])
+            send(block_of(p, 3, j), rb2.at[p, 1, j], (p, "b2-", j), down_of(p, 1))
+    for p in parts:
+        finish_line(p, 0)
+
+    def finish_block(p, j):
+        landed(rb2.at[p, 0, j], (p, "b2+", j))
+        landed(rb2.at[p, 1, j], (p, "b2-", j))
+        add_sub(sub(p, j), rb2.at[p, 0, j], rb2.at[p, 1, j])
+
+    for p in parts:
+        finish_block(p, 2)
+        send(sub(p, 2), rc1.at[p], (p, "c1"), device(dims[p][0], ahead))
+    for p in parts:
+        finish_block(p, 3)
+        finish_block(p, 1)
+        send(sub(p, behind), rc2.at[p, 0], (p, "c2"), device(dims[p][0], behind))
+    for p in parts:
+        landed(rc1.at[p], (p, "c1"))
+        add_sub(sub(p, ahead), rc1.at[p])
+        send(sub(p, ahead), rc2.at[p, 1], (p, "c3"), device(dims[p][0], ahead))
+    for p in parts:
+        finish_block(p, 0)
+    for p in parts:
+        landed(rc2.at[p, 0], (p, "c2"))
+        landed(rc2.at[p, 1], (p, "c3"))
+        total = (
+            sub(p, 0)[...].astype(jnp.float32)
+            + rc2[p, 0].astype(jnp.float32)
+            + rc2[p, 1].astype(jnp.float32)
+        )
+        width = min(PART, D - p * PART)
+        out[:, p * PART : p * PART + width] = total[:, :width]
+    for key, copy in pending.items():
+        if key not in waited:
+            copy.wait_send()
+    assert len(names.table) <= SENDS, len(names.table)
+
+
+def moe(x_in, gate, up, down):
+    bf = jnp.bfloat16
+    vmem = pl.BlockSpec(memory_space=pltpu.VMEM)
+    hbm = pl.BlockSpec(memory_space=pl.ANY)
+    return pl.pallas_call(
+        moe_kernel,
+        out_shape=jax.ShapeDtypeStruct((16, D), jnp.float32),
+        in_specs=[vmem, hbm, hbm, hbm],
+        out_specs=vmem,
+        scratch_shapes=[
+            pltpu.VMEM((3, 2, 4, 4, 4, 16, PART), bf),
+            pltpu.VMEM((3 * PART, 2 * HF), bf),
+            pltpu.VMEM((HF, 3 * PART), bf),
+            pltpu.VMEM((2, 4, 4, 4, 16, 2 * HF), jnp.float32),
+            pltpu.VMEM((2, 4, 4, 4, 16, HF), bf),
+            pltpu.VMEM((3, 4, 4, 4, 16, PART), bf),
+            pltpu.VMEM((3, 4, 4, 16, PART), bf),
+            pltpu.VMEM((3, 4, 4, 4, 16, PART), bf),
+            pltpu.VMEM((3, 2, 2, 4, 16, PART), bf),
+            pltpu.VMEM((3, 2, 4, 4, 16, PART), bf),
+            pltpu.VMEM((3, 2, 2, 16, PART), bf),
+            pltpu.VMEM((3, 2, 4, 16, PART), bf),
+            pltpu.VMEM((3, 16, PART), bf),
+            pltpu.VMEM((3, 2, 16, PART), bf),
+            pltpu.SemaphoreType.DMA((SENDS,)),
+            pltpu.SemaphoreType.DMA((SENDS,)),
+            pltpu.SemaphoreType.DMA((3,)),
+        ],
+        compiler_params=pltpu.CompilerParams(
+            collective_id=0, has_side_effects=True, vmem_limit_bytes=67043328
+        ),
+        name="moe",
+    )(x_in, gate, up, down)
 
 
 def local(
@@ -79,7 +484,6 @@
     up_slab,
     down_slab,
 ):
-    local_rows = resid.shape[0]
     attended = attend(queries, new_keys, new_values, cache_keys, cache_values, cache_len)
     regrouped = lax.all_to_all(attended, "ep", split_axis=1, concat_axis=0, tiled=True)
     attn_out = lax.psum_scatter(
@@ -99,39 +503,10 @@
     peak_logit = jnp.max(chosen, axis=1, keepdims=True)
     exp_logit = jnp.exp(chosen - peak_logit)
     gate_probs = (exp_logit / jnp.sum(exp_logit, axis=1, keepdims=True)).astype(jnp.bfloat16)
-    per_token = jnp.sum(onehot.astype(jnp.int32), axis=1)
-    before = jnp.cumsum(per_token, axis=0) - per_token
-    ranking = jnp.sum(jnp.where(onehot, before[:, None, :], 0), axis=2)
-    slab_count = lax.axis_size("ep") * lax.axis_size("dp")
-    half_slots = (4 * local_rows * TOP + 5 * experts - 1) // (5 * experts)
-    target = (2 * expert_ids + ranking % 2) * half_slots + ranking // 2
-    places = jnp.arange(slab_count * half_slots, dtype=jnp.int32)
-    slot_match = target[:, :, None] == places[None, None, :]
-    dispatch = jnp.any(slot_match, axis=1).astype(jnp.bfloat16)
-    combine = jnp.sum(
-        jnp.where(slot_match, gate_probs.astype(jnp.float32)[:, :, None], 0.0), axis=1
-    ).astype(jnp.bfloat16)
-    outgoing = lax.dot_general(
-        dispatch, normed, (((0,), (0,)), ((), ())), preferred_element_type=jnp.float32
-    )
-    outgoing = outgoing.astype(jnp.bfloat16).reshape(slab_count, half_slots, D)
-    partner = from_partner((gate_slab, up_slab, down_slab), "dp", 0)
-    incoming = lax.all_to_all(outgoing, ("ep", "dp"), split_axis=0, concat_axis=0, tiled=True)
-    sources, slot_count, feature_dim = incoming.shape
-    flat_rows = incoming.reshape(sources * slot_count, feature_dim)
-    produced = expert_ffn(flat_rows, gate_slab[0], up_slab[0], down_slab[0])
-    produced = produced + expert_ffn(flat_rows, partner[0][0], partner[1][0], partner[2][0])
-    returned = lax.all_to_all(
-        produced.astype(jnp.bfloat16).reshape(sources, slot_count, feature_dim),
-        ("ep", "dp"),
-        split_axis=0,
-        concat_axis=0,
-        tiled=True,
-    )
-    expert_mix = jnp.dot(
-        combine, returned.reshape(slab_count * half_slots, D), preferred_element_type=jnp.float32
-    )
-    return hidden + expert_mix
+    weights = jnp.sum(jnp.where(onehot, gate_probs.astype(jnp.float32)[:, :, None], 0.0), axis=1)
+    weights = jnp.pad(weights.astype(jnp.bfloat16), ((0, 0), (0, 3 * PART - D - experts)))
+    x_in = jnp.concatenate([normed, weights], axis=1)
+    return hidden + moe(x_in, gate_slab[0], up_slab[0], down_slab[0])
 
 
 def solution(mesh):

time: 359 us -> 259 us (0.72)
  waiting for transfers between devices: 244 us -> 78.4 us
  Pallas kernels: 0 us -> 131 us
  matrix products: 36.6 us -> 9.02 us
  starting transfers between devices: 23.4 us -> 0.01 us
  local copies, waits for them, and re-layouts: 20 us -> 2.88 us
    pallas_call x0 -> x1, Pallas kernels: none -> 131 us  [moe(): pl.pallas_call(moe_kernel, out_shape=jax.ShapeDtypeStruct((16, D), jnp.fl...]
    ppermute x3 -> x0, waiting for transfers between devices: 110 us -> none  [from_partner(): return lax.ppermute(value, axis, pairs)]
    all_to_all x2 -> x0, waiting for transfers between devices: 57.6 us -> none  [the longest x1 29.2 us: local(): lax.all_to_all(produced.astype(jnp.bfloat16).reshape(sources, slot_count,...]
    dot_general x6 -> x0, matrix products: 29.1 us -> none  [the longest x2 16.3 us: expert_ffn(): return jnp.dot(activated, down_part, preferred_element_type=jnp.float32)]
    all_to_all x2 -> x0, starting transfers between devices: 19.9 us -> none  [the longest x1 10 us: local(): lax.all_to_all(produced.astype(jnp.bfloat16).reshape(sources, slot_count,...]
    reshape x4 -> x0, local copies, waits for them, and re-layouts: 17 us -> none  [the longest x1 4.4 us: local(): outgoing = outgoing.astype(jnp.bfloat16).reshape(slab_count, half_slots, D)]
  transfers between devices with their start and end apart: 6 -> 1, of which waited for: 5 -> 1; matrix products, arithmetic and copies ran while one was open for 8% -> 0% of each run, Pallas kernels for 0% -> 0%
where the time goes in v1:
time: 259 us; the launch traced here: 258 us
  Pallas kernels  131 us (51%)
  waiting for transfers between devices  78.4 us (30%)
  blocking collectives  17.3 us (7%)
  between operations  13.5 us (5%)
  matrix products  9.02 us (3%)
  other arithmetic  6.2 us (2%)
  local copies, waits for them, and re-layouts  2.88 us (1%)
    pallas_call x1, Pallas kernels, moe(): pl.pallas_call(moe_kernel, out_shape=jax.ShapeDtypeStruct((16, D), jnp.fl...  131 us
    reduce_scatter x1, waiting for transfers between devices, local(): lax.psum_scatter(jnp.dot(regrouped, out_proj, preferred_element_type=jnp....  78.3 us
    all_to_all x1, blocking collectives, local(): lax.all_to_all(attended, 'ep', split_axis=1, concat_axis=0, tiled=True)  17.3 us
  transfers between devices with their start and end apart: 1, of which 1 were waited for; matrix products, arithmetic and copies ran while one was open for 0% of the time, Pallas kernels for 0%

profile of v1, /device:TPU:1, one launch (start us, length us, event | category | flops | bytes accessed | tf_op | source)
XLA Modules:
  0.0 258.2 jit_solution(12547032150493841683)
XLA Ops:
  6.5 0.0 reduce-scatter.2.cloned.1.call-start
  6.5 1.0 copy.40
  7.5 0.7 iota_compare_fusion.2
  8.3 0.7 reshape.102
  9.0 0.2 fusion.29
  9.3 2.9 %fusion.28 = (f32[16,4,16]{2,1,0:T(4,128)S(1)}, f32[16,4,16,128]{3,2,1,0:T(8,128)S(1)}) fusion(bf16[16,4,16,128]{3,2,1,0:T(8,128)(2,1)S(1)} %bitcast.48, pred[16,128]{1,0:T(8,128)(4,1)S(1)} %iota_compare_fusion.2, bf16[16,128,512]{2,1,0:T(8,128)(2,1)} %param.18), kind=kOutput, calls=%fused_computation.37 | convolution fusion | flops 33946624 | bytes 2889728 | tf_op jit(solution)/shard_map/tgqd,tcgd->tgqc/dot_general | solution.py:32
  12.2 0.4 fusion.18
  12.7 0.0 copy-done.3
  12.7 0.0 copy-start
  12.7 2.5 fusion.15
  15.2 0.1 convert_element_type.65
  15.3 0.2 copy.30
  15.4 17.3 %all_to_all.16 = bf16[16,32,256]{2,0,1:T(8,128)(2,1)S(1)} all-to-all(bf16[16,32,256]{2,0,1:T(8,128)(2,1)S(1)} %copy.30), channel_id=1, replica_groups=mesh['ep'=32,'dp'=4] {'ep'}, dimensions={1} | all-to-all | bytes 524288 | tf_op jit(solution)/shard_map/all_to_all | solution.py:488
  32.7 0.0 copy-done
  32.7 3.2 %convolution_convert_fusion = bf16[512,4096]{1,0:T(8,128)(2,1)} fusion(bf16[512,256]{1,0:T(8,128)(2,1)S(1)} %bitcast.49, bf16[256,4096]{1,0:T(8,128)(2,1)S(1)} %copy-done), kind=kOutput, calls=%fused_computation | convolution fusion | flops 1075838976 | bytes 6553600 | tf_op jit(solution)/shard_map/dot_general | solution.py:490
  35.9 0.0 reduce-scatter.2.cloned.1.call-update
  35.9 0.7 copy-done.5
  36.5 0.1 copy.31
  36.6 78.3 %reduce-scatter.2.cloned.1.call-done = bf16[16,4096]{1,0:T(8,128)(2,1)} async-done(((bf16[512,4096]{1,0:T(8,128)(2,1)}), bf16[16,4096]{1,0:T(8,128)(2,1)}) %reduce-scatter.2.cloned.1.call-update) | async-done | bytes 131088 | tf_op jit(solution)/shard_map/reduce_scatter | solution.py:489
  115.0 0.0 copy-done.1
  115.0 1.1 multiply_reduce_fusion
  116.0 0.0 copy-done.4
  116.0 1.0 multiply_convert_fusion
  117.1 0.2 fusion.30
  117.3 0.2 select_reduce_fusion.1
  117.5 0.1 copy.33
  117.5 0.1 reduce_max.19
  117.7 0.1 copy.34
  117.8 0.1 select_reduce_fusion
  117.9 0.7 fusion.23.x_in
  118.6 131.0 %moe.1 = f32[16,4096]{1,0:T(8,128)} custom-call(bf16[16,4224]{1,0:T(8,128)(2,1)} %fusion.23.x_in, bf16[4096,384]{1,0:T(8,128)(2,1)} %bitcast.44, bf16[4096,384]{1,0:T(8,128)(2,1)} %bitcast.45, bf16[384,4096]{1,0:T(8,128)(2,1)} %bitcast.46), custom_call_target="tpu_custom_call" | custom-call | tf_op jit(solution)/shard_map/moe/pallas_call | solution.py:440
  249.6 1.8 fusion.22
  (12 shorter events, 0.1 us)
Async XLA Ops:
  6.5 108.4 %reduce-scatter.2.cloned.1.call-start = ((), (), s32[]{:S(2)}) async-start(), calls=%async_computation.2 | async-start | bytes 4325376 | tf_op jit(solution)/shard_map/reduce_scatter | solution.py:489
  8.3 4.4 %copy-start.3 = (bf16[16,512]{1,0:T(8,128)(2,1)S(1)}, bf16[16,512]{1,0:T(8,128)(2,1)}, u32[]{:S(2)}) copy-start(bf16[16,512]{1,0:T(8,128)(2,1)} %param.17) | copy-start | bytes 49156
  12.7 20.0 %copy-start = (bf16[256,4096]{1,0:T(8,128)(2,1)S(1)}, bf16[256,4096]{1,0:T(8,128)(2,1)}, u32[]{:S(2)}) copy-start(bf16[256,4096]{1,0:T(8,128)(2,1)} %param.21) | copy-start | bytes 6291460
  35.9 0.7 copy-start.5
  35.9 79.1 %copy-start.1 = (bf16[16,4096]{1,0:T(8,128)(2,1)S(1)}, bf16[16,4096]{1,0:T(8,128)(2,1)}, u32[]{:S(2)}) copy-start(bf16[16,4096]{1,0:T(8,128)(2,1)} %param.14) | copy-start | bytes 393220
  35.9 80.2 %copy-start.4 = (f32[4096]{0:T(1024)S(1)}, f32[4096]{0:T(1024)}, u32[]{:S(2)}) copy-start(f32[4096]{0:T(1024)} %param.22) | copy-start | bytes 49156
  35.9 81.2 %copy-start.2 = (bf16[4096,64]{0,1:T(8,128)(2,1)S(1)}, bf16[4096,64]{0,1:T(8,128)(2,1)}, u32[]{:S(2)}) copy-start(bf16[4096,64]{0,1:T(8,128)(2,1)} %param.23) | copy-start | bytes 1572868
Sparse Core Ops, SparseCore 0:
  36.0 78.8 reduce-scatter.1

commit v2 on v1

--- a/solution.py
+++ b/solution.py
@@ -94,15 +94,13 @@
 
 def moe_kernel(
     x_in, gate, up, down, out,
-    rows, gu, dn, acc, act, part, pair_out, pair_in, ra1, ra2, rb1, rb2, rc1, rc2,
+    rows, gu, dn, acc, act, part, pair_out, pair_in, ra1, ra2, rb1, rb2, rc,
     send_sem, recv_sem, load_sem,
 ):
     here = Place()
     c = here.c
     other = 1 - c
     rel, device = here.rel, here.device
-    ahead = 1 + 2 * c
-    behind = 3 - 2 * c
     names = Names()
     pending = {}
 
@@ -131,7 +129,7 @@
 
     barrier = pltpu.get_barrier_semaphore()
     for dim in ("x", "y", "z"):
-        for o in (1, 3):
+        for o in (1, 2, 3):
             pl.semaphore_signal(barrier, inc=1, device_id=device(dim, o), device_id_type=MESH)
     pl.semaphore_signal(barrier, inc=1, device_id=device(other_core=True), device_id_type=MESH)
 
@@ -145,14 +143,14 @@
     mine = [x_in.at[:, pl.ds(p * PART, PART)] for p in range(3)]
     for p in range(3):
         rows[(p, c) + where(p, 0, 0, 0)] = x_in[:, p * PART : (p + 1) * PART]
-    pl.semaphore_wait(barrier, 7)
+    pl.semaphore_wait(barrier, 10)
 
     parts = range(3)
     dims = ORDER
     for p in parts:
         own = block(p, 0, 0, 0)
-        send(mine[p], own, (p, "1f"), device(dims[p][0], ahead))
-        send(mine[p], own, (p, "1b"), device(dims[p][0], behind))
+        for o in (1, 3, 2):
+            send(mine[p], own, (p, "1", o), device(dims[p][0], o))
     for p in parts:
         own = block(p, 0, 0, 0)
         send(mine[p], own, (p, "2+", 0), device(dims[p][1], 1))
@@ -180,14 +178,12 @@
         send(ref, ref, (p, "pair", o2, o3), device(other_core=True))
 
     for p in parts:
-        ref = block(p, behind, 0, 0)
-        landed(ref, (p, "1f"))
-        send(ref, ref, (p, "1g"), device(dims[p][0], ahead))
-        landed(block(p, ahead, 0, 0), (p, "1b"))
+        for o in (1, 3):
+            landed(block(p, 4 - o, 0, 0), (p, "1", o))
         send_sub(p, 1)
         send_sub(p, 3)
     for p in parts:
-        landed(block(p, 2, 0, 0), (p, "1g"))
+        landed(block(p, 2, 0, 0), (p, "1", 2))
         send_sub(p, 2)
         send_line(p, 0)
         pass_on(p, 0, 0)
@@ -214,48 +210,56 @@
         send_line(p, 2)
         pass_on(p, 2, 0)
 
-    def project(p, o2, o3):
-        landed(block(p, None, o2, o3, other), (p, "pair", o2, o3))
-        at = where(p, None, o2, o3)
-
-        @pl.loop(0, 3)
-        def _(n):
-            cols = pl.ds(pl.multiple_of(n * 256, 256), 256)
-            x = rows[(p, slice(None)) + at].reshape(128, PART)
-            y = jnp.dot(x, gu[p * PART : (p + 1) * PART, cols], preferred_element_type=jnp.float32)
-            idx = (slice(None),) + at + (slice(None), cols)
-            acc[idx] += y.reshape(2, 4, 16, 256)
-
-    seen = None
-    for j in (0, 1, 3, 2):
+    def project(*lines):
         for p in parts:
-            project(p, j, 0)
+            for o2, o3 in lines:
+                landed(block(p, None, o2, o3, other), (p, "pair", o2, o3))
+            at = [where(p, None, o2, o3) for o2, o3 in lines]
+
+            @pl.loop(0, 3)
+            def _(n):
+                cols = pl.ds(pl.multiple_of(n * 256, 256), 256)
+                x = [rows[(p, slice(None)) + a].reshape(128, PART) for a in at]
+                x = jnp.concatenate(x, axis=0)
+                w = gu[p * PART : (p + 1) * PART, cols]
+                y = jnp.dot(x, w, preferred_element_type=jnp.float32)
+                for i, a in enumerate(at):
+                    idx = (slice(None),) + a + (slice(None), cols)
+                    acc[idx] += y[i * 128 : (i + 1) * 128].reshape(2, 4, 16, 256)
+
+    def neighbours(j):
         for p in parts:
             ref = block(p, None, j, 3)
             landed(ref, (p, "3+", j))
-            if j in (0, 1):
+            if j in (0, 3):
                 send(ref, ref, (p, "3g", j), device(dims[p][2], 1))
             ref = block(p, None, j, 1)
             landed(ref, (p, "3-", j))
-            if j in (3, 2):
+            if j in (1, 2):
                 send(ref, ref, (p, "3g", j), device(dims[p][2], 3))
             pass_on(p, j, 3)
             pass_on(p, j, 1)
-        if seen is not None:
-            for p in parts:
-                project(p, seen, 3)
-                project(p, seen, 1)
-        seen = j
-    for p in parts:
-        project(p, seen, 3)
-        project(p, seen, 1)
-    for j in (0, 3, 1, 2):
+
+    def opposite(*lines):
         for p in parts:
-            landed(block(p, None, j, 2), (p, "3g", j))
-            pass_on(p, j, 2)
-    for j in (0, 3, 1, 2):
-        for p in parts:
-            project(p, j, 2)
+            for j in lines:
+                landed(block(p, None, j, 2), (p, "3g", j))
+                pass_on(p, j, 2)
+
+    project((0, 0), (1, 0))
+    neighbours(0)
+    project((3, 0), (2, 0))
+    neighbours(1)
+    project((0, 3), (0, 1))
+    neighbours(3)
+    project((1, 3), (1, 1))
+    neighbours(2)
+    project((3, 3), (3, 1))
+    opposite(0, 1)
+    project((2, 3), (2, 1))
+    opposite(3, 2)
+    project((0, 2), (1, 2))
+    project((3, 2), (2, 2))
 
     expert = lax.div(lax.axis_index("ep") * 4 + lax.axis_index("dp"), 2)
 
@@ -286,19 +290,23 @@
         at = {d: (rel(d, o1) if d == dims[p][2] else slice(None)) for d in "xyz"}
         return act[core, at["y"], at["x"], at["z"]].reshape(256, HF)
 
-    def product(p, o1, core, dst):
+    def product(p, o1):
+        def piece(cols, wcols, width):
+            h = jnp.concatenate([hidden_of(p, o1, other), hidden_of(p, o1, c)], axis=0)
+            y = jnp.dot(h, dn[:, wcols], preferred_element_type=jnp.float32).astype(jnp.bfloat16)
+            pair_out[p, :, :, :, cols] = y[:256].reshape(4, 4, 16, width)
+            part[p, o1, :, :, :, cols] = y[256:].reshape(4, 4, 16, width)
+
         @pl.loop(0, 5)
         def _(n):
-            cols = pl.ds(pl.multiple_of(n * 256, 256), 256)
-            wcols = pl.ds(pl.multiple_of(p * PART + n * 256, 128), 256)
-            y = jnp.dot(hidden_of(p, o1, core), dn[:, wcols], preferred_element_type=jnp.float32)
-            dst[:, :, :, cols] = y.astype(jnp.bfloat16).reshape(4, 4, 16, 256)
+            start = pl.multiple_of(n * 256, 256)
+            piece(pl.ds(start, 256), pl.ds(pl.multiple_of(p * PART + start, 128), 256), 256)
 
         if p < 2:
-            y = jnp.dot(hidden_of(p, o1, core), dn[:, p * PART + 1280 : (p + 1) * PART], preferred_element_type=jnp.float32)
-            dst[:, :, :, 1280:] = y.astype(jnp.bfloat16).reshape(4, 4, 16, 128)
+            piece(pl.ds(1280, 128), pl.ds(p * PART + 1280, 128), 128)
         else:
-            dst[:, :, :, 1280:] = jnp.zeros((4, 4, 16, 128), jnp.bfloat16)
+            pair_out[p, :, :, :, 1280:] = jnp.zeros((4, 4, 16, 128), jnp.bfloat16)
+            part[p, o1, :, :, :, 1280:] = jnp.zeros((4, 4, 16, 128), jnp.bfloat16)
 
     def add(dst, *srcs):
         @pl.loop(0, 4)
@@ -316,21 +324,26 @@
 
     waited = set()
 
-    def sums_for(o1):
+    def sums_for(o1, then):
+        def finish(p):
+            landed(pair_in.at[p, o1], (p, "sum", o1))
+
+            @pl.loop(0, 4)
+            def _(i):
+                add(part.at[p, o1, i], pair_in.at[p, o1, i])
+
+            then(p)
+
         for p in parts:
             for key in list(pending):
                 if key[:2] == (p, "sum") and key not in waited:
                     pending[key].wait_send()
                     waited.add(key)
-            product(p, o1, other, pair_out.at[p])
+            product(p, o1)
             send(pair_out.at[p], pair_in.at[p, o1], (p, "sum", o1), device(other_core=True))
-        for p in parts:
-            product(p, o1, c, part.at[p, o1])
-        for p in parts:
-            landed(pair_in.at[p, o1], (p, "sum", o1))
-            @pl.loop(0, 4)
-            def _(i):
-                add(part.at[p, o1, i], pair_in.at[p, o1, i])
+            if p:
+                finish(p - 1)
+        finish(2)
 
     def up_of(p, level):
         return device(dims[p][level], 1)
@@ -340,30 +353,30 @@
 
     UPWARD, DOWNWARD = (2, 1), (3, 0)
 
-    sums_for(2)
-    for k in range(2):
-        for p in parts:
+    def first(p):
+        for k in range(2):
             send(line(p, 2, UPWARD[k]), ra1.at[p, 0, k], (p, "a1+", k), up_of(p, 2))
             send(line(p, 2, DOWNWARD[k]), ra1.at[p, 1, k], (p, "a1-", k), down_of(p, 2))
-    sums_for(1)
-    for j in DOWNWARD:
+
+    def nothing(p):
+        pass
+
+    def second(direction, j):
         for p in parts:
-            send(line(p, 1, j), ra2.at[p, 0, j], (p, "a2+", j), up_of(p, 2))
-    sums_for(3)
-    for j in UPWARD:
-        for p in parts:
-            send(line(p, 3, j), ra2.at[p, 1, j], (p, "a2-", j), down_of(p, 2))
-    for k in range(2):
-        for p in parts:
-            j = UPWARD[k]
-            landed(ra1.at[p, 0, k], (p, "a1+", k))
-            add(line(p, 1, j), ra1.at[p, 0, k])
-            send(line(p, 1, j), ra2.at[p, 0, j], (p, "a2+", j), up_of(p, 2))
-            j = DOWNWARD[k]
-            landed(ra1.at[p, 1, k], (p, "a1-", k))
-            add(line(p, 3, j), ra1.at[p, 1, k])
-            send(line(p, 3, j), ra2.at[p, 1, j], (p, "a2-", j), down_of(p, 2))
-    sums_for(0)
+            o1, sign, joined = (1, "+", UPWARD) if direction == 0 else (3, "-", DOWNWARD)
+            if j in joined:
+                k = joined.index(j)
+                landed(ra1.at[p, direction, k], (p, "a1" + sign, k))
+                add(line(p, o1, j), ra1.at[p, direction, k])
+            send(line(p, o1, j), ra2.at[p, direction, j], (p, "a2" + sign, j), device(dims[p][2], o1))
+
+    sums_for(2, first)
+    sums_for(1, nothing)
+    sums_for(3, nothing)
+    for up_line, down_line in ((2, 2), (1, 3), (3, 1), (0, 0)):
+        second(0, up_line)
+        second(1, down_line)
+    sums_for(0, nothing)
 
     def finish_line(p, j):
         landed(ra2.at[p, 0, j], (p, "a2+", j))
@@ -404,27 +417,17 @@
         landed(rb2.at[p, 1, j], (p, "b2-", j))
         add_sub(sub(p, j), rb2.at[p, 0, j], rb2.at[p, 1, j])
 
-    for p in parts:
-        finish_block(p, 2)
-        send(sub(p, 2), rc1.at[p], (p, "c1"), device(dims[p][0], ahead))
-    for p in parts:
-        finish_block(p, 3)
-        finish_block(p, 1)
-        send(sub(p, behind), rc2.at[p, 0], (p, "c2"), device(dims[p][0], behind))
-    for p in parts:
-        landed(rc1.at[p], (p, "c1"))
-        add_sub(sub(p, ahead), rc1.at[p])
-        send(sub(p, ahead), rc2.at[p, 1], (p, "c3"), device(dims[p][0], ahead))
+    for o in (2, 3, 1):
+        for p in parts:
+            finish_block(p, o)
+            send(sub(p, o), rc.at[p, o - 1], (p, "c", o), device(dims[p][0], o))
     for p in parts:
         finish_block(p, 0)
     for p in parts:
-        landed(rc2.at[p, 0], (p, "c2"))
-        landed(rc2.at[p, 1], (p, "c3"))
-        total = (
-            sub(p, 0)[...].astype(jnp.float32)
-            + rc2[p, 0].astype(jnp.float32)
-            + rc2[p, 1].astype(jnp.float32)
-        )
+        total = sub(p, 0)[...].astype(jnp.float32)
+        for o in (3, 1, 2):
+            landed(rc.at[p, o - 1], (p, "c", o))
+            total += rc[p, o - 1].astype(jnp.float32)
         width = min(PART, D - p * PART)
         out[:, p * PART : p * PART + width] = total[:, :width]
     for key, copy in pending.items():
@@ -455,8 +458,7 @@
             pltpu.VMEM((3, 2, 4, 4, 16, PART), bf),
             pltpu.VMEM((3, 2, 2, 16, PART), bf),
             pltpu.VMEM((3, 2, 4, 16, PART), bf),
-            pltpu.VMEM((3, 16, PART), bf),
-            pltpu.VMEM((3, 2, 16, PART), bf),
+            pltpu.VMEM((3, 3, 16, PART), bf),
             pltpu.SemaphoreType.DMA((SENDS,)),
             pltpu.SemaphoreType.DMA((SENDS,)),
             pltpu.SemaphoreType.DMA((3,)),
@@ -466,6 +468,196 @@
         ),
         name="moe",
     )(x_in, gate, up, down)
+
+
+HALF = D // 2
+
+
+def project_kernel(
+    att, resid, gain, router, ids, w, hidden_out, x_out,
+    seen, part, pair_out, pair_in, ra1, ra2, rc,
+    send_sem, recv_sem, all_send, all_recv,
+):
+    here = Place()
+    c = here.c
+    other = 1 - c
+    rel, device = here.rel, here.device
+    ep, dp = lax.axis_index("ep"), lax.axis_index("dp")
+    names = Names()
+    pending = {}
+
+    def send(src, dst, key, dev):
+        i = names(*key)
+        copy = pltpu.make_async_remote_copy(
+            src_ref=src, dst_ref=dst, send_sem=send_sem.at[i], recv_sem=recv_sem.at[i],
+            device_id=dev, device_id_type=MESH,
+        )
+        copy.start()
+        pending[key] = copy
+
+    def landed(dst, key):
+        i = names(*key)
+        pltpu.make_async_remote_copy(
+            src_ref=dst, dst_ref=dst, send_sem=send_sem.at[i], recv_sem=recv_sem.at[i],
+            device_id=device(other_core=True), device_id_type=MESH,
+        ).wait_recv()
+
+    def slot(e):
+        return lax.rem(e, 2) * 16 + lax.div(e, 2)
+
+    barrier = pltpu.get_barrier_semaphore()
+    for k in range(1, 32):
+        pl.semaphore_signal(barrier, inc=1, device_id=(lax.rem(ep + k, 32), dp), device_id_type=MESH)
+    seen[slot(ep)] = att[:, pl.ds(pl.multiple_of(ep * 256, 256), 256)]
+    pl.semaphore_wait(barrier, 31)
+
+    for k in range(1, 32):
+        to = lax.rem(ep + k, 32)
+        pltpu.make_async_remote_copy(
+            src_ref=att.at[:, pl.ds(pl.multiple_of(to * 256, 256), 256)],
+            dst_ref=seen.at[slot(ep)],
+            send_sem=all_send.at[0],
+            recv_sem=all_recv.at[0],
+            device_id=(to, dp),
+            device_id_type=MESH,
+        ).start()
+    everything = pltpu.make_async_remote_copy(
+        src_ref=seen.at[pl.ds(0, 31)], dst_ref=seen.at[pl.ds(0, 31)],
+        send_sem=all_send.at[0], recv_sem=all_recv.at[0],
+        device_id=device(other_core=True), device_id_type=MESH,
+    )
+    everything.wait_recv()
+
+    first_dim = ("x", "y")
+    second_dim = ("y", "x")
+
+    def spot(q, o1, o2):
+        at = {first_dim[q]: rel(first_dim[q], o1), second_dim[q]: rel(second_dim[q], o2)}
+        return part.at[q, at["y"], at["x"]]
+
+    def product(q):
+        @pl.loop(0, HALF // 256)
+        def _(n):
+            start = pl.multiple_of(n * 256, 256)
+            theirs = seen[pl.ds(other * 16, 16)].reshape(256, 256)
+            ours = seen[pl.ds(c * 16, 16)].reshape(256, 256)
+            rows = jnp.concatenate([theirs, ours], axis=0)
+            cols = pl.ds(pl.multiple_of(q * HALF + start, 256), 256)
+            y = jnp.dot(rows, w[:, cols], preferred_element_type=jnp.float32).astype(jnp.bfloat16)
+            pair_out[q, :, :, :, pl.ds(start, 256)] = y[:256].reshape(4, 4, 16, 256)
+            part[q, :, :, :, pl.ds(start, 256)] = y[256:].reshape(4, 4, 16, 256)
+
+    def add(dst, *srcs):
+        total = dst[...].astype(jnp.float32)
+        for src in srcs:
+            total += src[...].astype(jnp.float32)
+        dst[...] = total.astype(jnp.bfloat16)
+
+    UPWARD, DOWNWARD = (2, 1), (3, 0)
+    for q in range(2):
+        product(q)
+        send(pair_out.at[q], pair_in.at[q], (q, "sum"), device(other_core=True))
+    for q in range(2):
+        landed(pair_in.at[q], (q, "sum"))
+
+        def join(o1, o2):
+            at = {first_dim[q]: rel(first_dim[q], o1), second_dim[q]: rel(second_dim[q], o2)}
+            add(spot(q, o1, o2), pair_in.at[q, at["y"], at["x"]])
+
+        for k in range(2):
+            join(2, UPWARD[k])
+            send(spot(q, 2, UPWARD[k]), ra1.at[q, 0, k], (q, "a1+", k), device(first_dim[q], 1))
+            join(2, DOWNWARD[k])
+            send(spot(q, 2, DOWNWARD[k]), ra1.at[q, 1, k], (q, "a1-", k), device(first_dim[q], 3))
+        for o1 in (1, 3, 0):
+            for o2 in range(4):
+                join(o1, o2)
+
+    def second(direction, j):
+        for q in range(2):
+            o1, sign, joined = (1, "+", UPWARD) if direction == 0 else (3, "-", DOWNWARD)
+            if j in joined:
+                k = joined.index(j)
+                landed(ra1.at[q, direction, k], (q, "a1" + sign, k))
+                add(spot(q, o1, j), ra1.at[q, direction, k])
+            send(spot(q, o1, j), ra2.at[q, direction, j], (q, "a2" + sign, j), device(first_dim[q], o1))
+
+    for up_block, down_block in ((3, 2), (2, 3), (1, 1), (0, 0)):
+        second(0, up_block)
+        second(1, down_block)
+
+    def finish(q, j):
+        landed(ra2.at[q, 0, j], (q, "a2+", j))
+        landed(ra2.at[q, 1, j], (q, "a2-", j))
+        add(spot(q, 0, j), ra2.at[q, 0, j], ra2.at[q, 1, j])
+
+    for o in (2, 3, 1):
+        for q in range(2):
+            finish(q, o)
+            send(spot(q, 0, o), rc.at[q, o - 1], (q, "c", o), device(second_dim[q], o))
+    for q in range(2):
+        finish(q, 0)
+    square = jnp.zeros((16, 1), jnp.float32)
+    for q in range(2):
+        total = spot(q, 0, 0)[...].astype(jnp.float32)
+        for o in (3, 1, 2):
+            landed(rc.at[q, o - 1], (q, "c", o))
+            total += rc[q, o - 1].astype(jnp.float32)
+        cols = slice(q * HALF, (q + 1) * HALF)
+        hidden = resid[:, cols].astype(jnp.float32) + total
+        hidden_out[:, cols] = hidden
+        square += jnp.sum(hidden * hidden, axis=1, keepdims=True)
+    scale = lax.rsqrt(jnp.maximum(square * (1.0 / D), 0.25))
+    logits = jnp.zeros((16, router.shape[1]), jnp.float32)
+    for q in range(2):
+        cols = slice(q * HALF, (q + 1) * HALF)
+        normed = (hidden_out[:, cols] * scale * gain[:, cols]).astype(jnp.bfloat16)
+        x_out[:, cols] = normed
+        logits += jnp.dot(normed, router[cols, :], preferred_element_type=jnp.float32)
+    labels = lax.broadcasted_iota(jnp.int32, logits.shape, 1)
+    named = ids[:, 0:1] == labels
+    for k in range(1, TOP):
+        named = named | (ids[:, k : k + 1] == labels)
+    peak = jnp.max(jnp.where(named, logits, -jnp.inf), axis=1, keepdims=True)
+    grown = jnp.where(named, jnp.exp(jnp.where(named, logits - peak, 0.0)), 0.0)
+    probs = grown / jnp.sum(grown, axis=1, keepdims=True)
+    rest = jnp.zeros((16, 3 * PART - D - router.shape[1]), jnp.float32)
+    x_out[:, D:] = jnp.concatenate([probs, rest], axis=1).astype(jnp.bfloat16)
+
+    everything.wait_send()
+    for copy in pending.values():
+        copy.wait_send()
+
+
+def attention_out(attended, resid, norm_gain, router, expert_ids, out_proj):
+    bf = jnp.bfloat16
+    vmem = pl.BlockSpec(memory_space=pltpu.VMEM)
+    return pl.pallas_call(
+        project_kernel,
+        out_shape=(
+            jax.ShapeDtypeStruct((16, D), jnp.float32),
+            jax.ShapeDtypeStruct((16, 3 * PART), bf),
+        ),
+        in_specs=[vmem] * 6,
+        out_specs=(vmem, vmem),
+        scratch_shapes=[
+            pltpu.VMEM((32, 16, 256), bf),
+            pltpu.VMEM((2, 4, 4, 16, HALF), bf),
+            pltpu.VMEM((2, 4, 4, 16, HALF), bf),
+            pltpu.VMEM((2, 4, 4, 16, HALF), bf),
+            pltpu.VMEM((2, 2, 2, 16, HALF), bf),
+            pltpu.VMEM((2, 2, 4, 16, HALF), bf),
+            pltpu.VMEM((2, 3, 16, HALF), bf),
+            pltpu.SemaphoreType.DMA((40,)),
+            pltpu.SemaphoreType.DMA((40,)),
+            pltpu.SemaphoreType.DMA((1,)),
+            pltpu.SemaphoreType.DMA((1,)),
+        ],
+        compiler_params=pltpu.CompilerParams(
+            collective_id=1, has_side_effects=True, vmem_limit_bytes=40 * 2**20
+        ),
+        name="attention_out",
+    )(attended, resid, norm_gain.reshape(1, D), router, expert_ids, out_proj)
 
 
 def local(
@@ -485,27 +677,7 @@
     down_slab,
 ):
     attended = attend(queries, new_keys, new_values, cache_keys, cache_values, cache_len)
-    regrouped = lax.all_to_all(attended, "ep", split_axis=1, concat_axis=0, tiled=True)
-    attn_out = lax.psum_scatter(
-        jnp.dot(regrouped, out_proj, preferred_element_type=jnp.float32).astype(jnp.bfloat16),
-        "ep",
-        scatter_dimension=0,
-        tiled=True,
-    ).astype(jnp.float32)
-    hidden = resid.astype(jnp.float32) + attn_out
-    meansq = jnp.mean(hidden * hidden, axis=1, keepdims=True)
-    normed = (hidden * lax.rsqrt(jnp.maximum(meansq, 0.25)) * norm_gain).astype(jnp.bfloat16)
-    logits = jnp.dot(normed, router, preferred_element_type=jnp.float32)
-    experts = router.shape[1]
-    labels = jnp.arange(experts, dtype=jnp.int32)
-    onehot = expert_ids[:, :, None] == labels[None, None, :]
-    chosen = jnp.sum(jnp.where(onehot, logits[:, None, :], 0.0), axis=2)
-    peak_logit = jnp.max(chosen, axis=1, keepdims=True)
-    exp_logit = jnp.exp(chosen - peak_logit)
-    gate_probs = (exp_logit / jnp.sum(exp_logit, axis=1, keepdims=True)).astype(jnp.bfloat16)
-    weights = jnp.sum(jnp.where(onehot, gate_probs.astype(jnp.float32)[:, :, None], 0.0), axis=1)
-    weights = jnp.pad(weights.astype(jnp.bfloat16), ((0, 0), (0, 3 * PART - D - experts)))
-    x_in = jnp.concatenate([normed, weights], axis=1)
+    hidden, x_in = attention_out(attended, resid, norm_gain, router, expert_ids, out_proj)
     return hidden + moe(x_in, gate_slab[0], up_slab[0], down_slab[0])
 
 

time: 259 us -> 159 us (0.61)
  waiting for transfers between devices: 78.4 us -> 0 us
  blocking collectives: 17.3 us -> 0 us
  between operations: 13.5 us -> 0.12 us
  Pallas kernels: 131 us -> 144 us
  matrix products: 9.02 us -> 4.03 us
  local copies, waits for them, and re-layouts: 2.88 us -> 7.11 us
  other arithmetic: 6.2 us -> 2.97 us
    reduce_scatter x1 -> x0, waiting for transfers between devices: 78.3 us -> none  [local(): lax.psum_scatter(jnp.dot(regrouped, out_proj, preferred_element_type=jnp....]
    pallas_call x0 -> x1, Pallas kernels: none -> 34.4 us  [attention_out(): pl.pallas_call(project_kernel, out_shape=(jax.ShapeDtypeStruct((16, D), j...]
    pallas_call x1, Pallas kernels: 131 us -> 110 us  [moe(): pl.pallas_call(moe_kernel, out_shape=jax.ShapeDtypeStruct((16, D), jnp.fl...]
    all_to_all x1 -> x0, blocking collectives: 17.3 us -> none  [local(): lax.all_to_all(attended, 'ep', split_axis=1, concat_axis=0, tiled=True)]
    unnamed x14 -> x16, local copies, waits for them, and re-layouts: 1.74 us -> 5.64 us
    dot_general x2 -> x0, matrix products: 3.43 us -> none  [the longest x1 3.19 us: local(): jnp.dot(regrouped, out_proj, preferred_element_type=jnp.float32)]
  transfers between devices with their start and end apart: 1 -> 0, of which waited for: 1 -> 0; matrix products, arithmetic and copies ran while one was open for 0% -> 0% of each run, Pallas kernels for 0% -> 0%
where the time goes in v2:
time: 159 us; the launch traced here: 158 us
  Pallas kernels  144 us (91%)
  local copies, waits for them, and re-layouts  7.11 us (4%)
  matrix products  4.03 us (3%)
  other arithmetic  2.97 us (2%)
    pallas_call x1, Pallas kernels, moe(): pl.pallas_call(moe_kernel, out_shape=jax.ShapeDtypeStruct((16, D), jnp.fl...  110 us
    pallas_call x1, Pallas kernels, attention_out(): pl.pallas_call(project_kernel, out_shape=(jax.ShapeDtypeStruct((16, D), j...  34.4 us
    unnamed x16, local copies, waits for them, and re-layouts  5.64 us

profile of v2, /device:TPU:1, one launch (start us, length us, event | category | flops | bytes accessed | tf_op | source)
XLA Modules:
  0.0 158.2 jit_solution(15415247288127567136)
XLA Ops:
  0.0 0.7 iota_compare_fusion
  0.7 0.8 copy.18.ids
  1.5 0.7 reshape.54
  2.2 0.7 reshape.50
  3.0 1.0 copy.23
  4.0 0.0 copy-start.5
  4.0 0.2 fusion.24
  4.2 3.0 %fusion.23 = (f32[16,4,16]{2,1,0:T(4,128)S(1)}, f32[16,4,16,128]{3,2,1,0:T(8,128)S(1)}) fusion(bf16[16,4,16,128]{3,2,1,0:T(8,128)(2,1)S(1)} %bitcast.47, pred[16,128]{1,0:T(8,128)(4,1)S(1)} %iota_compare_fusion, bf16[16,128,512]{2,1,0:T(8,128)(2,1)} %param.18), kind=kOutput, calls=%fused_computation.22 | convolution fusion | flops 33946624 | bytes 2889728 | tf_op jit(solution)/shard_map/tgqd,tcgd->tgqc/dot_general | solution.py:32
  7.3 0.4 fusion.18
  7.7 0.0 copy-done.5
  7.8 0.0 copy-start.3
  7.8 0.8 fusion.15
  8.5 0.0 copy-start
  8.5 0.2 copy.44
  8.7 1.6 %copy.17.router = bf16[4096,64]{1,0:T(8,128)(2,1)S(1)} copy(bf16[4096,64]{0,1:T(8,128)(2,1)} %param.23) | data formatting | bytes 1048576 | tf_op args[9]
  10.3 0.0 copy-done.3
  10.4 0.0 copy-done
  10.4 0.0 copy-start.4
  10.4 0.7 copy-done.4
  11.1 34.4 %attention_out.1 = (f32[16,4096]{1,0:T(8,128)S(1)}, bf16[16,4224]{1,0:T(8,128)(2,1)S(1)}) custom-call(bf16[16,8192]{1,0:T(8,128)(2,1)S(1)} %bitcast.41, bf16[16,4096]{1,0:T(8,128)(2,1)S(1)} %copy-done.3, f32[1,4096]{1,0:T(1,128)S(1)} %bitcast.42, bf16[4096,64]{1,0:T(8,128)(2,1)S(1)} %copy.17.router, s32[16,8]{1,0:T(8,128)S(1)} %copy.18.ids, ...), custom_call_target="tpu_custom_call" | custom-call | tf_op jit(solution)/shard_map/attention_out/pallas_call | solution.py:635
  45.5 0.0 copy-start.1
  45.5 0.7 copy-done.1
  46.2 0.0 copy-start.2
  46.2 0.7 copy-done.2
  46.8 109.6 %moe.1 = f32[16,4096]{1,0:T(8,128)} custom-call(bf16[16,4224]{1,0:T(8,128)(2,1)} %copy-done.2, bf16[4096,384]{1,0:T(8,128)(2,1)} %bitcast.43, bf16[4096,384]{1,0:T(8,128)(2,1)} %bitcast.44, bf16[384,4096]{1,0:T(8,128)(2,1)} %bitcast.45), custom_call_target="tpu_custom_call" | custom-call | tf_op jit(solution)/shard_map/moe/pallas_call | solution.py:443
  156.5 1.8 %add.11 = f32[16,4096]{1,0:T(8,128)} add(f32[16,4096]{1,0:T(8,128)} %copy-done.1, f32[16,4096]{1,0:T(8,128)} %moe.1) | non-fusion elementwise | flops 65536 | bytes 786432 | tf_op jit(solution)/shard_map/add | solution.py:681
  (2 shorter events, 0.1 us)
Async XLA Ops:
  4.0 3.8 %copy-start.5 = (bf16[16,128,512]{2,1,0:T(8,128)(2,1)S(1)}, bf16[16,128,512]{2,1,0:T(8,128)(2,1)}, u32[]{:S(2)}) copy-start(bf16[16,128,512]{2,1,0:T(8,128)(2,1)} %param.19) | copy-start | bytes 6291460
  7.8 2.6 %copy-start.3 = (bf16[16,4096]{1,0:T(8,128)(2,1)S(1)}, bf16[16,4096]{1,0:T(8,128)(2,1)}, u32[]{:S(2)}) copy-start(bf16[16,4096]{1,0:T(8,128)(2,1)} %resid.1) | copy-start | bytes 393220
  8.5 1.8 %copy-start = (bf16[256,4096]{1,0:T(8,128)(2,1)S(1)}, bf16[256,4096]{1,0:T(8,128)(2,1)}, u32[]{:S(2)}) copy-start(bf16[256,4096]{1,0:T(8,128)(2,1)} %w.1) | copy-start | bytes 6291460
  10.4 0.7 copy-start.4
  45.5 0.7 copy-start.1
  46.2 0.7 copy-start.2

commit v3 on v2

--- a/solution.py
+++ b/solution.py
@@ -89,12 +89,13 @@
         return self.table.setdefault(key, len(self.table))
 
 
-SENDS = 260
+GROUPS = ("1", "2", "2g", "3", "3g", "pair", "a1", "a2", "b1", "b2", "c", ("sum", 0), ("sum", 1), ("sum", 2))
+KEYS = 126
 
 
 def moe_kernel(
-    x_in, gate, up, down, out,
-    rows, gu, dn, acc, act, part, pair_out, pair_in, ra1, ra2, rb1, rb2, rc,
+    x_in, hidden, gate, up, down, out,
+    residual, rows, gu, dn, acc, act, part, pair_out, pair_in, ra1, ra2, rb1, rb2, rc,
     send_sem, recv_sem, load_sem,
 ):
     here = Place()
@@ -102,23 +103,37 @@
     other = 1 - c
     rel, device = here.rel, here.device
     names = Names()
-    pending = {}
-
-    def send(src, dst, key, dev):
-        i = names(*key)
+    parts = range(3)
+    dims = ORDER
+
+    def send(src, dst, key, dev, group):
         copy = pltpu.make_async_remote_copy(
-            src_ref=src, dst_ref=dst, send_sem=send_sem.at[i], recv_sem=recv_sem.at[i],
+            src_ref=src, dst_ref=dst, send_sem=send_sem.at[GROUPS.index(group)], recv_sem=recv_sem.at[names(*key)],
             device_id=dev, device_id_type=MESH,
         )
         copy.start()
-        pending[key] = copy
-
-    def landed(dst, key):
-        i = names(*key)
+        return copy
+
+    def landed(ref, key):
         pltpu.make_async_remote_copy(
-            src_ref=dst, dst_ref=dst, send_sem=send_sem.at[i], recv_sem=recv_sem.at[i],
+            src_ref=ref, dst_ref=ref, send_sem=send_sem.at[0], recv_sem=recv_sem.at[names(*key)],
             device_id=device(other_core=True), device_id_type=MESH,
         ).wait_recv()
+
+    def sent(ref, group):
+        pltpu.make_async_remote_copy(
+            src_ref=ref, dst_ref=ref, send_sem=send_sem.at[GROUPS.index(group)], recv_sem=recv_sem.at[0],
+            device_id=device(other_core=True), device_id_type=MESH,
+        ).wait_send()
+
+    def amount(p, n):
+        if n == 1:
+            return rows.at[p, 0, 0, 0, 0]
+        if n < 4:
+            return rows.at[p, 0, 0, 0, pl.ds(0, n)]
+        if n < 16:
+            return rows.at[p, 0, 0, pl.ds(0, n // 4)]
+        return rows.at[p, 0, pl.ds(0, n // 16)]
 
     def where(p, o1, o2, o3):
         at = {d: (slice(None) if o is None else rel(d, o)) for d, o in zip(ORDER[p], (o1, o2, o3))}
@@ -126,6 +141,30 @@
 
     def block(p, o1, o2, o3, core=None):
         return rows.at[(p, c if core is None else core) + where(p, o1, o2, o3)]
+
+    def send_sub(p, j):
+        ref = block(p, j, 0, 0)
+        send(ref, ref, (p, "2", j), device(dims[p][1], 1), "2")
+        send(ref, ref, (p, "2", j), device(dims[p][1], 3), "2")
+
+    def send_line(p, j):
+        ref = block(p, None, j, 0)
+        send(ref, ref, (p, "3", j), device(dims[p][2], 1), "3")
+        send(ref, ref, (p, "3", j), device(dims[p][2], 3), "3")
+
+    def send_block(p, i, j):
+        ref = block(p, i, j, 0)
+        send(ref, ref, (p, "3", j), device(dims[p][2], 1), "3")
+        send(ref, ref, (p, "3", j), device(dims[p][2], 3), "3")
+
+    def unit(o2, o3):
+        if o3 in (1, 3):
+            return "near", o2
+        return o3, o2 in (0, 1)
+
+    def pass_on(p, o2, o3):
+        ref = block(p, None, o2, o3)
+        send(ref, ref, (p, "pair") + unit(o2, o3), device(other_core=True), "pair")
 
     barrier = pltpu.get_barrier_semaphore()
     for dim in ("x", "y", "z"):
@@ -133,6 +172,14 @@
             pl.semaphore_signal(barrier, inc=1, device_id=device(dim, o), device_id_type=MESH)
     pl.semaphore_signal(barrier, inc=1, device_id=device(other_core=True), device_id_type=MESH)
 
+    fetch = pltpu.make_async_copy(hidden, residual, load_sem.at[3])
+    fetch.start()
+    starts = [
+        pltpu.make_async_copy(x_in.at[:, pl.ds(p * PART, PART)], rows.at[(p, c) + where(p, 0, 0, 0)], load_sem.at[4 + p])
+        for p in range(3)
+    ]
+    for copy in starts:
+        copy.start()
     loads = [
         pltpu.make_async_copy(gate, gu.at[pl.ds(0, D), pl.ds(0, HF)], load_sem.at[0]),
         pltpu.make_async_copy(up, gu.at[pl.ds(0, D), pl.ds(HF, HF)], load_sem.at[1]),
@@ -140,21 +187,18 @@
     ]
     for copy in loads:
         copy.start()
-    mine = [x_in.at[:, pl.ds(p * PART, PART)] for p in range(3)]
-    for p in range(3):
-        rows[(p, c) + where(p, 0, 0, 0)] = x_in[:, p * PART : (p + 1) * PART]
     pl.semaphore_wait(barrier, 10)
 
-    parts = range(3)
-    dims = ORDER
+    for copy in starts:
+        copy.wait()
+    fetch.wait()
     for p in parts:
         own = block(p, 0, 0, 0)
-        for o in (1, 3, 2):
-            send(mine[p], own, (p, "1", o), device(dims[p][0], o))
-    for p in parts:
-        own = block(p, 0, 0, 0)
-        send(mine[p], own, (p, "2+", 0), device(dims[p][1], 1))
-        send(mine[p], own, (p, "2-", 0), device(dims[p][1], 3))
+        for o in (1, 3):
+            send(own, own, (p, "1n"), device(dims[p][0], o), "1")
+        send(own, own, (p, "1f"), device(dims[p][0], 2), "1")
+    for p in parts:
+        send_sub(p, 0)
 
     gu[D:, :] = jnp.zeros((3 * PART - D, 2 * HF), jnp.bfloat16)
     dn[:, D:] = jnp.zeros((HF, 3 * PART - D), jnp.bfloat16)
@@ -163,60 +207,43 @@
     def _(i):
         acc[i // 16, lax.rem(i, 16) // 4, lax.rem(i, 4)] = jnp.zeros((4, 16, 2 * HF), jnp.float32)
 
-    def send_sub(p, j):
-        ref = block(p, j, 0, 0)
-        send(ref, ref, (p, "2+", j), device(dims[p][1], 1))
-        send(ref, ref, (p, "2-", j), device(dims[p][1], 3))
-
-    def send_line(p, j):
-        ref = block(p, None, j, 0)
-        send(ref, ref, (p, "3+", j), device(dims[p][2], 1))
-        send(ref, ref, (p, "3-", j), device(dims[p][2], 3))
-
-    def pass_on(p, o2, o3):
-        ref = block(p, None, o2, o3)
-        send(ref, ref, (p, "pair", o2, o3), device(other_core=True))
-
-    for p in parts:
-        for o in (1, 3):
-            landed(block(p, 4 - o, 0, 0), (p, "1", o))
+    for p in parts:
+        send_block(p, 0, 0)
+    for p in parts:
+        landed(amount(p, 2), (p, "1n"))
         send_sub(p, 1)
         send_sub(p, 3)
     for p in parts:
-        landed(block(p, 2, 0, 0), (p, "1", 2))
+        landed(amount(p, 1), (p, "1f"))
         send_sub(p, 2)
-        send_line(p, 0)
+    for p in parts:
+        for i in (1, 3, 2):
+            send_block(p, i, 0)
         pass_on(p, 0, 0)
     for j in (0, 1, 3, 2):
         for p in parts:
-            ref = block(p, j, 3, 0)
-            landed(ref, (p, "2+", j))
-            if j in (0, 1):
-                send(ref, ref, (p, "2g", j), device(dims[p][1], 1))
-            ref = block(p, j, 1, 0)
-            landed(ref, (p, "2-", j))
-            if j in (3, 2):
-                send(ref, ref, (p, "2g", j), device(dims[p][1], 3))
-    for p in parts:
-        send_line(p, 1)
-        send_line(p, 3)
+            landed(amount(p, 2), (p, "2", j))
+            o = 3 if j in (0, 1) else 1
+            ref = block(p, j, o, 0)
+            send(ref, ref, (p, "2g"), device(dims[p][1], 4 - o), "2g")
+            send_block(p, j, 1)
+            send_block(p, j, 3)
+    for p in parts:
         pass_on(p, 1, 0)
         pass_on(p, 3, 0)
     for copy in loads:
         copy.wait()
     for p in parts:
-        for j in (0, 1, 3, 2):
-            landed(block(p, j, 2, 0), (p, "2g", j))
+        landed(amount(p, 4), (p, "2g"))
         send_line(p, 2)
         pass_on(p, 2, 0)
 
     def project(*lines):
         for p in parts:
-            for o2, o3 in lines:
-                landed(block(p, None, o2, o3, other), (p, "pair", o2, o3))
+            landed(amount(p, 8), (p, "pair") + unit(*lines[0]))
             at = [where(p, None, o2, o3) for o2, o3 in lines]
 
-            @pl.loop(0, 3)
+            @pl.loop(0, 3, unroll=3)
             def _(n):
                 cols = pl.ds(pl.multiple_of(n * 256, 256), 256)
                 x = [rows[(p, slice(None)) + a].reshape(128, PART) for a in at]
@@ -229,21 +256,17 @@
 
     def neighbours(j):
         for p in parts:
-            ref = block(p, None, j, 3)
-            landed(ref, (p, "3+", j))
-            if j in (0, 3):
-                send(ref, ref, (p, "3g", j), device(dims[p][2], 1))
-            ref = block(p, None, j, 1)
-            landed(ref, (p, "3-", j))
-            if j in (1, 2):
-                send(ref, ref, (p, "3g", j), device(dims[p][2], 3))
+            landed(amount(p, 8), (p, "3", j))
+            o = 3 if j in (0, 3) else 1
+            ref = block(p, None, j, o)
+            send(ref, ref, (p, "3g", j in (0, 1)), device(dims[p][2], 4 - o), "3g")
             pass_on(p, j, 3)
             pass_on(p, j, 1)
 
     def opposite(*lines):
         for p in parts:
+            landed(amount(p, 8), (p, "3g", lines[0] in (0, 1)))
             for j in lines:
-                landed(block(p, None, j, 2), (p, "3g", j))
                 pass_on(p, j, 2)
 
     project((0, 0), (1, 0))
@@ -263,11 +286,9 @@
 
     expert = lax.div(lax.axis_index("ep") * 4 + lax.axis_index("dp"), 2)
 
-    @pl.loop(0, 32)
-    def _(i):
-        at = (i // 16, lax.rem(i, 16) // 4, lax.rem(i, 4))
+    def activate(at):
         sums = acc[at].reshape(64, 2 * HF)
-        tail = rows[(2,) + at + (slice(None), slice(None), slice(PART - 128, PART))]
+        tail = rows[(2,) + at + (slice(None), slice(PART - 128, PART))]
         tail = tail.reshape(64, 128).astype(jnp.float32)
         lanes = lax.broadcasted_iota(jnp.int32, (64, 128), 1)
         prob = jnp.sum(jnp.where(lanes == expert, tail, 0.0), axis=1, keepdims=True)
@@ -275,6 +296,24 @@
         h = (g / (1.0 + jnp.exp(-g)) * u).astype(jnp.bfloat16).astype(jnp.float32) * prob
         act[at] = h.astype(jnp.bfloat16).reshape(4, 16, HF)
 
+    every = slice(None)
+
+    def activate_opposite(p):
+        far = rel(dims[p][2], 2)
+
+        @pl.loop(0, 8)
+        def _(i):
+            core, k = i // 4, lax.rem(i, 4)
+            activate(((core, k, every, far), (core, k, far, every), (core, far, k, every))[p])
+
+    def activate_rest():
+        @pl.loop(0, 18)
+        def _(i):
+            k = lax.rem(i, 9)
+            oy, ox = k // 3, lax.rem(k, 3)
+            oy, ox = oy + oy // 2, ox + ox // 2
+            activate((i // 9, rel("y", oy), rel("x", ox), every))
+
     def spot(p, o2, o3):
         a2 = slice(None) if o2 is None else rel(dims[p][1], o2)
         a3 = slice(None) if o3 is None else rel(dims[p][0], o3)
@@ -297,7 +336,7 @@
             pair_out[p, :, :, :, cols] = y[:256].reshape(4, 4, 16, width)
             part[p, o1, :, :, :, cols] = y[256:].reshape(4, 4, 16, width)
 
-        @pl.loop(0, 5)
+        @pl.loop(0, 5, unroll=5)
         def _(n):
             start = pl.multiple_of(n * 256, 256)
             piece(pl.ds(start, 256), pl.ds(pl.multiple_of(p * PART + start, 128), 256), 256)
@@ -322,9 +361,9 @@
             total += s[...].astype(jnp.float32)
         dst[...] = total.astype(jnp.bfloat16)
 
-    waited = set()
-
-    def sums_for(o1, then):
+    last = {}
+
+    def sums_for(o1, then, before=None):
         def finish(p):
             landed(pair_in.at[p, o1], (p, "sum", o1))
 
@@ -335,12 +374,12 @@
             then(p)
 
         for p in parts:
-            for key in list(pending):
-                if key[:2] == (p, "sum") and key not in waited:
-                    pending[key].wait_send()
-                    waited.add(key)
+            if p in last:
+                last[p].wait_send()
+            if before is not None:
+                before(p)
             product(p, o1)
-            send(pair_out.at[p], pair_in.at[p, o1], (p, "sum", o1), device(other_core=True))
+            last[p] = send(pair_out.at[p], pair_in.at[p, o1], (p, "sum", o1), device(other_core=True), ("sum", p))
             if p:
                 finish(p - 1)
         finish(2)
@@ -355,32 +394,35 @@
 
     def first(p):
         for k in range(2):
-            send(line(p, 2, UPWARD[k]), ra1.at[p, 0, k], (p, "a1+", k), up_of(p, 2))
-            send(line(p, 2, DOWNWARD[k]), ra1.at[p, 1, k], (p, "a1-", k), down_of(p, 2))
+            send(line(p, 2, UPWARD[k]), ra1.at[p, 0, k], (p, "a1", 0, k), up_of(p, 2), "a1")
+            send(line(p, 2, DOWNWARD[k]), ra1.at[p, 1, k], (p, "a1", 1, k), down_of(p, 2), "a1")
 
     def nothing(p):
         pass
 
     def second(direction, j):
+        o1, joined = (1, UPWARD) if direction == 0 else (3, DOWNWARD)
         for p in parts:
-            o1, sign, joined = (1, "+", UPWARD) if direction == 0 else (3, "-", DOWNWARD)
             if j in joined:
                 k = joined.index(j)
-                landed(ra1.at[p, direction, k], (p, "a1" + sign, k))
+                landed(ra1.at[p, direction, k], (p, "a1", direction, k))
                 add(line(p, o1, j), ra1.at[p, direction, k])
-            send(line(p, o1, j), ra2.at[p, direction, j], (p, "a2" + sign, j), device(dims[p][2], o1))
-
-    sums_for(2, first)
+            send(line(p, o1, j), ra2.at[p, direction, j], (p, "a2", j), device(dims[p][2], o1), "a2")
+
+    sums_for(2, first, activate_opposite)
+    activate_rest()
     sums_for(1, nothing)
     sums_for(3, nothing)
-    for up_line, down_line in ((2, 2), (1, 3), (3, 1), (0, 0)):
-        second(0, up_line)
-        second(1, down_line)
+    second(0, 2)
+    second(1, 2)
+    second(0, 1)
+    second(1, 3)
+    second(0, 3)
+    second(1, 1)
     sums_for(0, nothing)
 
     def finish_line(p, j):
-        landed(ra2.at[p, 0, j], (p, "a2+", j))
-        landed(ra2.at[p, 1, j], (p, "a2-", j))
+        landed(ra2.at[p, 0, pl.ds(0, 2)], (p, "a2", j))
         add(line(p, 0, j), ra2.at[p, 0, j], ra2.at[p, 1, j])
 
     def block_of(p, o2, o3):
@@ -389,63 +431,69 @@
     for p in parts:
         finish_line(p, 2)
         for k in range(2):
-            send(block_of(p, 2, UPWARD[k]), rb1.at[p, 0, k], (p, "b1+", k), up_of(p, 1))
-            send(block_of(p, 2, DOWNWARD[k]), rb1.at[p, 1, k], (p, "b1-", k), down_of(p, 1))
+            send(block_of(p, 2, UPWARD[k]), rb1.at[p, 0, k], (p, "b1", 0, k), up_of(p, 1), "b1")
+            send(block_of(p, 2, DOWNWARD[k]), rb1.at[p, 1, k], (p, "b1", 1, k), down_of(p, 1), "b1")
+    second(0, 0)
+    second(1, 0)
     for p in parts:
         finish_line(p, 3)
         for j in UPWARD:
-            send(block_of(p, 3, j), rb2.at[p, 1, j], (p, "b2-", j), down_of(p, 1))
+            send(block_of(p, 3, j), rb2.at[p, 1, j], (p, "b2", j), down_of(p, 1), "b2")
     for p in parts:
         finish_line(p, 1)
         for j in DOWNWARD:
-            send(block_of(p, 1, j), rb2.at[p, 0, j], (p, "b2+", j), up_of(p, 1))
+            send(block_of(p, 1, j), rb2.at[p, 0, j], (p, "b2", j), up_of(p, 1), "b2")
     for k in range(2):
         for p in parts:
             j = UPWARD[k]
-            landed(rb1.at[p, 0, k], (p, "b1+", k))
+            landed(rb1.at[p, 0, k], (p, "b1", 0, k))
             add_sub(block_of(p, 1, j), rb1.at[p, 0, k])
-            send(block_of(p, 1, j), rb2.at[p, 0, j], (p, "b2+", j), up_of(p, 1))
+            send(block_of(p, 1, j), rb2.at[p, 0, j], (p, "b2", j), up_of(p, 1), "b2")
             j = DOWNWARD[k]
-            landed(rb1.at[p, 1, k], (p, "b1-", k))
+            landed(rb1.at[p, 1, k], (p, "b1", 1, k))
             add_sub(block_of(p, 3, j), rb1.at[p, 1, k])
-            send(block_of(p, 3, j), rb2.at[p, 1, j], (p, "b2-", j), down_of(p, 1))
+            send(block_of(p, 3, j), rb2.at[p, 1, j], (p, "b2", j), down_of(p, 1), "b2")
     for p in parts:
         finish_line(p, 0)
 
     def finish_block(p, j):
-        landed(rb2.at[p, 0, j], (p, "b2+", j))
-        landed(rb2.at[p, 1, j], (p, "b2-", j))
+        landed(rb2.at[p, 0, pl.ds(0, 2)], (p, "b2", j))
         add_sub(sub(p, j), rb2.at[p, 0, j], rb2.at[p, 1, j])
 
     for o in (2, 3, 1):
         for p in parts:
             finish_block(p, o)
-            send(sub(p, o), rc.at[p, o - 1], (p, "c", o), device(dims[p][0], o))
+            send(sub(p, o), rc.at[p, o - 1], (p, "c"), device(dims[p][0], o), "c")
     for p in parts:
         finish_block(p, 0)
     for p in parts:
+        landed(rc.at[p], (p, "c"))
         total = sub(p, 0)[...].astype(jnp.float32)
         for o in (3, 1, 2):
-            landed(rc.at[p, o - 1], (p, "c", o))
             total += rc[p, o - 1].astype(jnp.float32)
         width = min(PART, D - p * PART)
-        out[:, p * PART : p * PART + width] = total[:, :width]
-    for key, copy in pending.items():
-        if key not in waited:
-            copy.wait_send()
-    assert len(names.table) <= SENDS, len(names.table)
-
-
-def moe(x_in, gate, up, down):
+        cols = slice(p * PART, p * PART + width)
+        out[:, cols] = residual[:, cols] + total[:, :width]
+    for group, n in (("1", 3), ("2", 8), ("2g", 4), ("3", 32), ("3g", 16), ("pair", 64)):
+        sent(amount(slice(None), n), group)
+    for group, n in (("a1", 16), ("a2", 32), ("b1", 4), ("b2", 8), ("c", 3)):
+        sent(amount(slice(None), n), group)
+    for p in parts:
+        last[p].wait_send()
+    assert len(names.table) == KEYS, len(names.table)
+
+
+def moe(x_in, hidden, gate, up, down):
     bf = jnp.bfloat16
     vmem = pl.BlockSpec(memory_space=pltpu.VMEM)
     hbm = pl.BlockSpec(memory_space=pl.ANY)
     return pl.pallas_call(
         moe_kernel,
         out_shape=jax.ShapeDtypeStruct((16, D), jnp.float32),
-        in_specs=[vmem, hbm, hbm, hbm],
+        in_specs=[hbm] * 5,
         out_specs=vmem,
         scratch_shapes=[
+            pltpu.VMEM((16, D), jnp.float32),
             pltpu.VMEM((3, 2, 4, 4, 4, 16, PART), bf),
             pltpu.VMEM((3 * PART, 2 * HF), bf),
             pltpu.VMEM((HF, 3 * PART), bf),
@@ -459,24 +507,24 @@
             pltpu.VMEM((3, 2, 2, 16, PART), bf),
             pltpu.VMEM((3, 2, 4, 16, PART), bf),
             pltpu.VMEM((3, 3, 16, PART), bf),
-            pltpu.SemaphoreType.DMA((SENDS,)),
-            pltpu.SemaphoreType.DMA((SENDS,)),
-            pltpu.SemaphoreType.DMA((3,)),
+            pltpu.SemaphoreType.DMA((len(GROUPS),)),
+            pltpu.SemaphoreType.DMA((KEYS,)),
+            pltpu.SemaphoreType.DMA((7,)),
         ],
         compiler_params=pltpu.CompilerParams(
             collective_id=0, has_side_effects=True, vmem_limit_bytes=67043328
         ),
         name="moe",
-    )(x_in, gate, up, down)
+    )(x_in, hidden, gate, up, down)
 
 
 HALF = D // 2
 
 
 def project_kernel(
-    att, resid, gain, router, ids, w, hidden_out, x_out,
-    seen, part, pair_out, pair_in, ra1, ra2, rc,
-    send_sem, recv_sem, all_send, all_recv,
+    att, resid_hbm, gain_hbm, router_hbm, ids_hbm, w_hbm, hidden_out, x_out,
+    resid, gain, router, ids, w, seen, part, pair_out, pair_in, ra1, ra2, rc,
+    send_sem, recv_sem, all_send, all_recv, load_sem,
 ):
     here = Place()
     c = here.c
@@ -484,23 +532,33 @@
     rel, device = here.rel, here.device
     ep, dp = lax.axis_index("ep"), lax.axis_index("dp")
     names = Names()
-    pending = {}
+    groups = ("sum", "a1", "a2", "c")
+    loads = [
+        pltpu.make_async_copy(src, dst, load_sem.at[i])
+        for i, (src, dst) in enumerate(
+            ((w_hbm, w), (resid_hbm, resid), (gain_hbm, gain), (router_hbm, router), (ids_hbm, ids))
+        )
+    ]
+    for copy in loads:
+        copy.start()
 
     def send(src, dst, key, dev):
-        i = names(*key)
-        copy = pltpu.make_async_remote_copy(
-            src_ref=src, dst_ref=dst, send_sem=send_sem.at[i], recv_sem=recv_sem.at[i],
+        pltpu.make_async_remote_copy(
+            src_ref=src, dst_ref=dst, send_sem=send_sem.at[groups.index(key[1])], recv_sem=recv_sem.at[names(*key)],
             device_id=dev, device_id_type=MESH,
-        )
-        copy.start()
-        pending[key] = copy
-
-    def landed(dst, key):
-        i = names(*key)
+        ).start()
+
+    def landed(ref, key):
         pltpu.make_async_remote_copy(
-            src_ref=dst, dst_ref=dst, send_sem=send_sem.at[i], recv_sem=recv_sem.at[i],
+            src_ref=ref, dst_ref=ref, send_sem=send_sem.at[0], recv_sem=recv_sem.at[names(*key)],
             device_id=device(other_core=True), device_id_type=MESH,
         ).wait_recv()
+
+    def sent(ref, group):
+        pltpu.make_async_remote_copy(
+            src_ref=ref, dst_ref=ref, send_sem=send_sem.at[groups.index(group)], recv_sem=recv_sem.at[0],
+            device_id=device(other_core=True), device_id_type=MESH,
+        ).wait_send()
 
     def slot(e):
         return lax.rem(e, 2) * 16 + lax.div(e, 2)
@@ -526,6 +584,7 @@
         send_sem=all_send.at[0], recv_sem=all_recv.at[0],
         device_id=device(other_core=True), device_id_type=MESH,
     )
+    loads[0].wait()
     everything.wait_recv()
 
     first_dim = ("x", "y")
@@ -536,7 +595,7 @@
         return part.at[q, at["y"], at["x"]]
 
     def product(q):
-        @pl.loop(0, HALF // 256)
+        @pl.loop(0, HALF // 256, unroll=4)
         def _(n):
             start = pl.multiple_of(n * 256, 256)
             theirs = seen[pl.ds(other * 16, 16)].reshape(256, 256)
@@ -566,67 +625,78 @@
 
         for k in range(2):
             join(2, UPWARD[k])
-            send(spot(q, 2, UPWARD[k]), ra1.at[q, 0, k], (q, "a1+", k), device(first_dim[q], 1))
+            send(spot(q, 2, UPWARD[k]), ra1.at[q, 0, k], (q, "a1", 0, k), device(first_dim[q], 1))
             join(2, DOWNWARD[k])
-            send(spot(q, 2, DOWNWARD[k]), ra1.at[q, 1, k], (q, "a1-", k), device(first_dim[q], 3))
+            send(spot(q, 2, DOWNWARD[k]), ra1.at[q, 1, k], (q, "a1", 1, k), device(first_dim[q], 3))
         for o1 in (1, 3, 0):
             for o2 in range(4):
                 join(o1, o2)
 
     def second(direction, j):
         for q in range(2):
-            o1, sign, joined = (1, "+", UPWARD) if direction == 0 else (3, "-", DOWNWARD)
+            o1, joined = (1, UPWARD) if direction == 0 else (3, DOWNWARD)
             if j in joined:
                 k = joined.index(j)
-                landed(ra1.at[q, direction, k], (q, "a1" + sign, k))
+                landed(ra1.at[q, direction, k], (q, "a1", direction, k))
                 add(spot(q, o1, j), ra1.at[q, direction, k])
-            send(spot(q, o1, j), ra2.at[q, direction, j], (q, "a2" + sign, j), device(first_dim[q], o1))
+            send(spot(q, o1, j), ra2.at[q, direction, j], (q, "a2", j), device(first_dim[q], o1))
 
     for up_block, down_block in ((3, 2), (2, 3), (1, 1), (0, 0)):
         second(0, up_block)
         second(1, down_block)
 
     def finish(q, j):
-        landed(ra2.at[q, 0, j], (q, "a2+", j))
-        landed(ra2.at[q, 1, j], (q, "a2-", j))
+        landed(ra2.at[q, 0, pl.ds(0, 2)], (q, "a2", j))
         add(spot(q, 0, j), ra2.at[q, 0, j], ra2.at[q, 1, j])
 
     for o in (2, 3, 1):
         for q in range(2):
             finish(q, o)
-            send(spot(q, 0, o), rc.at[q, o - 1], (q, "c", o), device(second_dim[q], o))
+            send(spot(q, 0, o), rc.at[q, o - 1], (q, "c"), device(second_dim[q], o))
     for q in range(2):
         finish(q, 0)
+    for copy in loads[1:]:
+        copy.wait()
     square = jnp.zeros((16, 1), jnp.float32)
     for q in range(2):
+        landed(rc.at[q], (q, "c"))
         total = spot(q, 0, 0)[...].astype(jnp.float32)
         for o in (3, 1, 2):
-            landed(rc.at[q, o - 1], (q, "c", o))
             total += rc[q, o - 1].astype(jnp.float32)
         cols = slice(q * HALF, (q + 1) * HALF)
         hidden = resid[:, cols].astype(jnp.float32) + total
         hidden_out[:, cols] = hidden
         square += jnp.sum(hidden * hidden, axis=1, keepdims=True)
     scale = lax.rsqrt(jnp.maximum(square * (1.0 / D), 0.25))
-    logits = jnp.zeros((16, router.shape[1]), jnp.float32)
+    logits = jnp.zeros((router.shape[0], 16), jnp.float32)
     for q in range(2):
         cols = slice(q * HALF, (q + 1) * HALF)
         normed = (hidden_out[:, cols] * scale * gain[:, cols]).astype(jnp.bfloat16)
         x_out[:, cols] = normed
-        logits += jnp.dot(normed, router[cols, :], preferred_element_type=jnp.float32)
-    labels = lax.broadcasted_iota(jnp.int32, logits.shape, 1)
-    named = ids[:, 0:1] == labels
+        logits += lax.dot_general(
+            router[:, cols], normed, (((1,), (1,)), ((), ())), preferred_element_type=jnp.float32
+        )
+    labels = lax.broadcasted_iota(jnp.int32, logits.shape, 0)
+    named = ids[0:1, :] == labels
     for k in range(1, TOP):
-        named = named | (ids[:, k : k + 1] == labels)
-    peak = jnp.max(jnp.where(named, logits, -jnp.inf), axis=1, keepdims=True)
+        named = named | (ids[k : k + 1, :] == labels)
+    peak = jnp.max(jnp.where(named, logits, -jnp.inf), axis=0, keepdims=True)
     grown = jnp.where(named, jnp.exp(jnp.where(named, logits - peak, 0.0)), 0.0)
-    probs = grown / jnp.sum(grown, axis=1, keepdims=True)
-    rest = jnp.zeros((16, 3 * PART - D - router.shape[1]), jnp.float32)
-    x_out[:, D:] = jnp.concatenate([probs, rest], axis=1).astype(jnp.bfloat16)
+    probs = (grown / jnp.sum(grown, axis=0, keepdims=True)).astype(jnp.bfloat16)
+    experts = router.shape[0]
+    spread = (experts, 3 * PART - D)
+    ones = lax.broadcasted_iota(jnp.int32, spread, 0) == lax.broadcasted_iota(jnp.int32, spread, 1)
+    x_out[:, D:] = lax.dot_general(
+        probs, ones.astype(jnp.float32).astype(jnp.bfloat16), (((0,), (0,)), ((), ())),
+        preferred_element_type=jnp.float32,
+    ).astype(jnp.bfloat16)
 
     everything.wait_send()
-    for copy in pending.values():
-        copy.wait_send()
+    sent(pair_out, "sum")
+    sent(part.at[0, pl.ds(0, 2)], "a1")
+    sent(part.at[0], "a2")
+    sent(part.at[:, 0, pl.ds(0, 3)], "c")
+    assert len(names.table) == 20
 
 
 def attention_out(attended, resid, norm_gain, router, expert_ids, out_proj):
@@ -638,9 +708,14 @@
             jax.ShapeDtypeStruct((16, D), jnp.float32),
             jax.ShapeDtypeStruct((16, 3 * PART), bf),
         ),
-        in_specs=[vmem] * 6,
+        in_specs=[vmem] + [pl.BlockSpec(memory_space=pl.ANY)] * 5,
         out_specs=(vmem, vmem),
         scratch_shapes=[
+            pltpu.VMEM((16, D), bf),
+            pltpu.VMEM((1, D), jnp.float32),
+            pltpu.VMEM(router.shape[::-1], bf),
+            pltpu.VMEM((TOP, 16), jnp.int32),
+            pltpu.VMEM((256, D), bf),
             pltpu.VMEM((32, 16, 256), bf),
             pltpu.VMEM((2, 4, 4, 16, HALF), bf),
             pltpu.VMEM((2, 4, 4, 16, HALF), bf),
@@ -648,16 +723,17 @@
             pltpu.VMEM((2, 2, 2, 16, HALF), bf),
             pltpu.VMEM((2, 2, 4, 16, HALF), bf),
             pltpu.VMEM((2, 3, 16, HALF), bf),
-            pltpu.SemaphoreType.DMA((40,)),
-            pltpu.SemaphoreType.DMA((40,)),
+            pltpu.SemaphoreType.DMA((4,)),
+            pltpu.SemaphoreType.DMA((20,)),
             pltpu.SemaphoreType.DMA((1,)),
             pltpu.SemaphoreType.DMA((1,)),
+            pltpu.SemaphoreType.DMA((5,)),
         ],
         compiler_params=pltpu.CompilerParams(
-            collective_id=1, has_side_effects=True, vmem_limit_bytes=40 * 2**20
+            collective_id=1, has_side_effects=True, vmem_limit_bytes=67043328
         ),
         name="attention_out",
-    )(attended, resid, norm_gain.reshape(1, D), router, expert_ids, out_proj)
+    )(attended, resid, norm_gain.reshape(1, D), router.T, expert_ids.T, out_proj)
 
 
 def local(
@@ -678,7 +754,7 @@
 ):
     attended = attend(queries, new_keys, new_values, cache_keys, cache_values, cache_len)
     hidden, x_in = attention_out(attended, resid, norm_gain, router, expert_ids, out_proj)
-    return hidden + moe(x_in, gate_slab[0], up_slab[0], down_slab[0])
+    return moe(x_in, hidden, gate_slab[0], up_slab[0], down_slab[0])
 
 
 def solution(mesh):

time: 159 us -> 149 us (0.937)
  Pallas kernels: 144 us -> 138 us
  local copies, waits for them, and re-layouts: 7.11 us -> 5.02 us
  other arithmetic: 2.97 us -> 1.21 us
    pallas_call x1, Pallas kernels: 110 us -> 104 us  [moe(): pl.pallas_call(moe_kernel, out_shape=jax.ShapeDtypeStruct((16, D), jnp.fl...]
    unnamed x16 -> x5, local copies, waits for them, and re-layouts: 5.64 us -> 3.55 us
    add x1 -> x0, other arithmetic: 1.76 us -> none  [local(): return hidden + moe(x_in, gate_slab[0], up_slab[0], down_slab[0])]
where the time goes in v3:
time: 149 us; the launch traced here: 148 us
  Pallas kernels  138 us (93%)
  local copies, waits for them, and re-layouts  5.02 us (3%)
  matrix products  4.03 us (3%)
    pallas_call x1, Pallas kernels, moe(): pl.pallas_call(moe_kernel, out_shape=jax.ShapeDtypeStruct((16, D), jnp.fl...  104 us
    pallas_call x1, Pallas kernels, attention_out(): pl.pallas_call(project_kernel, out_shape=(jax.ShapeDtypeStruct((16, D), j...  34.4 us
    unnamed x5, local copies, waits for them, and re-layouts  3.55 us
    dot_general x1, matrix products, attend(): jnp.einsum('tgqd,tcgd->tgqc', query_heads, past_keys, preferred_element_t...  3.03 us

profile of v3, /device:TPU:1, one launch (start us, length us, event | category | flops | bytes accessed | tf_op | source)
XLA Modules:
  0.0 148.5 jit_solution(3973666810937662123)
XLA Ops:
  0.0 0.7 iota_compare_fusion
  0.7 0.7 reshape.54
  1.5 0.7 reshape.50
  2.2 1.0 copy.21
  3.2 0.0 copy-start
  3.2 0.2 fusion.24
  3.5 3.0 %fusion.23 = (f32[16,4,16]{2,1,0:T(4,128)S(1)}, f32[16,4,16,128]{3,2,1,0:T(8,128)S(1)}) fusion(bf16[16,4,16,128]{3,2,1,0:T(8,128)(2,1)S(1)} %bitcast.47, pred[16,128]{1,0:T(8,128)(4,1)S(1)} %iota_compare_fusion, bf16[16,128,512]{2,1,0:T(8,128)(2,1)} %param.18), kind=kOutput, calls=%fused_computation.22 | convolution fusion | flops 33946624 | bytes 2889728 | tf_op jit(solution)/shard_map/tgqd,tcgd->tgqc/dot_general | solution.py:32
  6.5 0.4 fusion.18
  7.0 0.0 copy-done
  7.0 0.8 fusion.15
  7.8 0.9 copy.42
  8.6 34.4 %attention_out.1 = (f32[16,4096]{1,0:T(8,128)}, bf16[16,4224]{1,0:T(8,128)(2,1)}) custom-call(bf16[16,8192]{1,0:T(8,128)(2,1)} %bitcast.48, bf16[16,4096]{1,0:T(8,128)(2,1)} %resid_hbm.1, f32[1,4096]{1,0:T(1,128)} %bitcast.54, bf16[64,4096]{1,0:T(8,128)(2,1)} %bitcast.49, s32[8,16]{1,0:T(8,128)} %bitcast.55, bf16[256,4096]{1,0:T(8,128)(2,1)} %w_hbm.1), custom_call_target="tpu_custom_call" | custom-call | tf_op jit(solution)/shard_map/attention_out/pallas_call | solution.py:705
  43.0 103.8 %moe.1 = f32[16,4096]{1,0:T(8,128)} custom-call(bf16[16,4224]{1,0:T(8,128)(2,1)} %get-tuple-element.7.x_in, f32[16,4096]{1,0:T(8,128)} %get-tuple-element.8.hidden, bf16[4096,384]{1,0:T(8,128)(2,1)} %bitcast.43, bf16[4096,384]{1,0:T(8,128)(2,1)} %bitcast.44, bf16[384,4096]{1,0:T(8,128)(2,1)} %bitcast.45), custom_call_target="tpu_custom_call" | custom-call | tf_op jit(solution)/shard_map/moe/pallas_call | solution.py:490
  146.8 1.7 %copy.44 = f32[16,4096]{1,0:T(8,128)} copy(f32[16,4096]{1,0:T(8,128)} %moe.1) | data formatting | bytes 524288
  (2 shorter events, 0.1 us)
Async XLA Ops:
  3.2 3.8 %copy-start = (bf16[16,128,512]{2,1,0:T(8,128)(2,1)S(1)}, bf16[16,128,512]{2,1,0:T(8,128)(2,1)}, u32[]{:S(2)}) copy-start(bf16[16,128,512]{2,1,0:T(8,128)(2,1)} %param.19) | copy-start | bytes 6291460

commit v4 on v3

--- a/solution.py
+++ b/solution.py
@@ -90,7 +90,7 @@
 
 
 GROUPS = ("1", "2", "2g", "3", "3g", "pair", "a1", "a2", "b1", "b2", "c", ("sum", 0), ("sum", 1), ("sum", 2))
-KEYS = 126
+KEYS = 129
 
 
 def moe_kernel(
@@ -160,11 +160,29 @@
     def unit(o2, o3):
         if o3 in (1, 3):
             return "near", o2
-        return o3, o2 in (0, 1)
+        if o3 == 0:
+            return "own", (0, 1, 2, 1)[o2]
+        return "far", o2 in (0, 1)
 
     def pass_on(p, o2, o3):
         ref = block(p, None, o2, o3)
         send(ref, ref, (p, "pair") + unit(o2, o3), device(other_core=True), "pair")
+
+    def project(*lines):
+        for p in parts:
+            landed(amount(p, 4 * len(lines)), (p, "pair") + unit(*lines[0]))
+            at = [where(p, None, o2, o3) for o2, o3 in lines]
+
+            @pl.loop(0, 3, unroll=3)
+            def _(n):
+                cols = pl.ds(pl.multiple_of(n * 256, 256), 256)
+                x = [rows[(p, slice(None)) + a].reshape(128, PART) for a in at]
+                x = jnp.concatenate(x, axis=0)
+                w = gu[p * PART : (p + 1) * PART, cols]
+                y = jnp.dot(x, w, preferred_element_type=jnp.float32)
+                for i, a in enumerate(at):
+                    idx = (slice(None),) + a + (slice(None), cols)
+                    acc[idx] += y[i * 128 : (i + 1) * 128].reshape(2, 4, 16, 256)
 
     barrier = pltpu.get_barrier_semaphore()
     for dim in ("x", "y", "z"):
@@ -220,6 +238,9 @@
         for i in (1, 3, 2):
             send_block(p, i, 0)
         pass_on(p, 0, 0)
+    for copy in loads:
+        copy.wait()
+    project((0, 0))
     for j in (0, 1, 3, 2):
         for p in parts:
             landed(amount(p, 2), (p, "2", j))
@@ -231,28 +252,11 @@
     for p in parts:
         pass_on(p, 1, 0)
         pass_on(p, 3, 0)
-    for copy in loads:
-        copy.wait()
+    project((1, 0), (3, 0))
     for p in parts:
         landed(amount(p, 4), (p, "2g"))
         send_line(p, 2)
         pass_on(p, 2, 0)
-
-    def project(*lines):
-        for p in parts:
-            landed(amount(p, 8), (p, "pair") + unit(*lines[0]))
-            at = [where(p, None, o2, o3) for o2, o3 in lines]
-
-            @pl.loop(0, 3, unroll=3)
-            def _(n):
-                cols = pl.ds(pl.multiple_of(n * 256, 256), 256)
-                x = [rows[(p, slice(None)) + a].reshape(128, PART) for a in at]
-                x = jnp.concatenate(x, axis=0)
-                w = gu[p * PART : (p + 1) * PART, cols]
-                y = jnp.dot(x, w, preferred_element_type=jnp.float32)
-                for i, a in enumerate(at):
-                    idx = (slice(None),) + a + (slice(None), cols)
-                    acc[idx] += y[i * 128 : (i + 1) * 128].reshape(2, 4, 16, 256)
 
     def neighbours(j):
         for p in parts:
@@ -269,9 +273,8 @@
             for j in lines:
                 pass_on(p, j, 2)
 
-    project((0, 0), (1, 0))
     neighbours(0)
-    project((3, 0), (2, 0))
+    project((2, 0))
     neighbours(1)
     project((0, 3), (0, 1))
     neighbours(3)
@@ -293,7 +296,7 @@
         lanes = lax.broadcasted_iota(jnp.int32, (64, 128), 1)
         prob = jnp.sum(jnp.where(lanes == expert, tail, 0.0), axis=1, keepdims=True)
         g, u = sums[:, :HF], sums[:, HF:]
-        h = (g / (1.0 + jnp.exp(-g)) * u).astype(jnp.bfloat16).astype(jnp.float32) * prob
+        h = (g * (0.5 + 0.5 * jnp.tanh(0.5 * g)) * u).astype(jnp.bfloat16).astype(jnp.float32) * prob
         act[at] = h.astype(jnp.bfloat16).reshape(4, 16, HF)
 
     every = slice(None)
@@ -615,22 +618,26 @@
     UPWARD, DOWNWARD = (2, 1), (3, 0)
     for q in range(2):
         product(q)
-        send(pair_out.at[q], pair_in.at[q], (q, "sum"), device(other_core=True))
-    for q in range(2):
-        landed(pair_in.at[q], (q, "sum"))
-
-        def join(o1, o2):
-            at = {first_dim[q]: rel(first_dim[q], o1), second_dim[q]: rel(second_dim[q], o2)}
-            add(spot(q, o1, o2), pair_in.at[q, at["y"], at["x"]])
-
-        for k in range(2):
-            join(2, UPWARD[k])
-            send(spot(q, 2, UPWARD[k]), ra1.at[q, 0, k], (q, "a1", 0, k), device(first_dim[q], 1))
-            join(2, DOWNWARD[k])
-            send(spot(q, 2, DOWNWARD[k]), ra1.at[q, 1, k], (q, "a1", 1, k), device(first_dim[q], 3))
-        for o1 in (1, 3, 0):
-            for o2 in range(4):
-                join(o1, o2)
+    for o1 in (2, 1, 3, 0):
+        for q in range(2):
+            far = rel(first_dim[q], o1)
+            mine = (q, slice(None), far) if q == 0 else (q, far)
+            send(pair_out.at[mine], pair_in.at[mine], (q, "sum", o1), device(other_core=True))
+
+    def join(o1):
+        for q in range(2):
+            landed(pair_in.at[q, 0], (q, "sum", o1))
+            for o2 in (2, 3, 1, 0):
+                at = {first_dim[q]: rel(first_dim[q], o1), second_dim[q]: rel(second_dim[q], o2)}
+                add(spot(q, o1, o2), pair_in.at[q, at["y"], at["x"]])
+                if o1 == 2:
+                    way = 0 if o2 in UPWARD else 1
+                    n = (UPWARD, DOWNWARD)[way].index(o2)
+                    send(spot(q, 2, o2), ra1.at[q, way, n], (q, "a1", way, n), device(first_dim[q], 1 + 2 * way))
+
+    join(2)
+    join(1)
+    join(3)
 
     def second(direction, j):
         for q in range(2):
@@ -644,6 +651,7 @@
     for up_block, down_block in ((3, 2), (2, 3), (1, 1), (0, 0)):
         second(0, up_block)
         second(1, down_block)
+    join(0)
 
     def finish(q, j):
         landed(ra2.at[q, 0, pl.ds(0, 2)], (q, "a2", j))
@@ -696,7 +704,7 @@
     sent(part.at[0, pl.ds(0, 2)], "a1")
     sent(part.at[0], "a2")
     sent(part.at[:, 0, pl.ds(0, 3)], "c")
-    assert len(names.table) == 20
+    assert len(names.table) == 26
 
 
 def attention_out(attended, resid, norm_gain, router, expert_ids, out_proj):
@@ -724,7 +732,7 @@
             pltpu.VMEM((2, 2, 4, 16, HALF), bf),
             pltpu.VMEM((2, 3, 16, HALF), bf),
             pltpu.SemaphoreType.DMA((4,)),
-            pltpu.SemaphoreType.DMA((20,)),
+            pltpu.SemaphoreType.DMA((26,)),
             pltpu.SemaphoreType.DMA((1,)),
             pltpu.SemaphoreType.DMA((1,)),
             pltpu.SemaphoreType.DMA((5,)),

time: 149 us -> 143 us (0.960)
  Pallas kernels: 138 us -> 132 us
    pallas_call x1, Pallas kernels: 104 us -> 98.7 us  [moe(): pl.pallas_call(moe_kernel, out_shape=jax.ShapeDtypeStruct((16, D), jnp.fl...]
where the time goes in v4:
time: 143 us; the launch traced here: 142 us
  Pallas kernels  132 us (92%)
  local copies, waits for them, and re-layouts  5.02 us (4%)
  matrix products  4.03 us (3%)
    pallas_call x1, Pallas kernels, moe(): pl.pallas_call(moe_kernel, out_shape=jax.ShapeDtypeStruct((16, D), jnp.fl...  98.7 us
    pallas_call x1, Pallas kernels, attention_out(): pl.pallas_call(project_kernel, out_shape=(jax.ShapeDtypeStruct((16, D), j...  33.2 us
    unnamed x5, local copies, waits for them, and re-layouts  3.55 us
    dot_general x1, matrix products, attend(): jnp.einsum('tgqd,tcgd->tgqc', query_heads, past_keys, preferred_element_t...  3.03 us

profile of v4, /device:TPU:1, one launch (start us, length us, event | category | flops | bytes accessed | tf_op | source)
XLA Modules:
  0.0 142.2 jit_solution(12843723002061775314)
XLA Ops:
  0.0 0.7 iota_compare_fusion
  0.7 0.7 reshape.54
  1.5 0.7 reshape.50
  2.2 1.0 copy.21
  3.2 0.0 copy-start
  3.2 0.2 fusion.24
  3.5 3.0 %fusion.23 = (f32[16,4,16]{2,1,0:T(4,128)S(1)}, f32[16,4,16,128]{3,2,1,0:T(8,128)S(1)}) fusion(bf16[16,4,16,128]{3,2,1,0:T(8,128)(2,1)S(1)} %bitcast.47, pred[16,128]{1,0:T(8,128)(4,1)S(1)} %iota_compare_fusion, bf16[16,128,512]{2,1,0:T(8,128)(2,1)} %param.18), kind=kOutput, calls=%fused_computation.22 | convolution fusion | flops 33946624 | bytes 2889728 | tf_op jit(solution)/shard_map/tgqd,tcgd->tgqc/dot_general | solution.py:32
  6.5 0.4 fusion.18
  7.0 0.0 copy-done
  7.0 0.8 fusion.15
  7.8 0.9 copy.42
  8.6 33.2 %attention_out.1 = (f32[16,4096]{1,0:T(8,128)}, bf16[16,4224]{1,0:T(8,128)(2,1)}) custom-call(bf16[16,8192]{1,0:T(8,128)(2,1)} %bitcast.48, bf16[16,4096]{1,0:T(8,128)(2,1)} %resid_hbm.1, f32[1,4096]{1,0:T(1,128)} %bitcast.54, bf16[64,4096]{1,0:T(8,128)(2,1)} %bitcast.49, s32[8,16]{1,0:T(8,128)} %bitcast.55, bf16[256,4096]{1,0:T(8,128)(2,1)} %w_hbm.1), custom_call_target="tpu_custom_call" | custom-call | tf_op jit(solution)/shard_map/attention_out/pallas_call | solution.py:713
  41.8 98.7 %moe.1 = f32[16,4096]{1,0:T(8,128)} custom-call(bf16[16,4224]{1,0:T(8,128)(2,1)} %get-tuple-element.7.x_in, f32[16,4096]{1,0:T(8,128)} %get-tuple-element.8.hidden, bf16[4096,384]{1,0:T(8,128)(2,1)} %bitcast.43, bf16[4096,384]{1,0:T(8,128)(2,1)} %bitcast.44, bf16[384,4096]{1,0:T(8,128)(2,1)} %bitcast.45), custom_call_target="tpu_custom_call" | custom-call | tf_op jit(solution)/shard_map/moe/pallas_call | solution.py:493
  140.6 1.7 %copy.44 = f32[16,4096]{1,0:T(8,128)} copy(f32[16,4096]{1,0:T(8,128)} %moe.1) | data formatting | bytes 524288
  (2 shorter events, 0.0 us)
Async XLA Ops:
  3.2 3.8 %copy-start = (bf16[16,128,512]{2,1,0:T(8,128)(2,1)S(1)}, bf16[16,128,512]{2,1,0:T(8,128)(2,1)}, u32[]{:S(2)}) copy-start(bf16[16,128,512]{2,1,0:T(8,128)(2,1)} %param.19) | copy-start | bytes 6291460

commit v5 on v4

--- a/solution.py
+++ b/solution.py
@@ -20,42 +20,37 @@
 HF = 384
 
 
-def attend(queries, new_keys, new_values, cache_keys, cache_values, cache_len):
-    local_rows = queries.shape[0]
-    cache_span = cache_keys.shape[1]
-    group_size = H // KVH
-    query_heads = queries.reshape(local_rows, KVH, group_size, HD)
-    past_keys = cache_keys.reshape(local_rows, cache_span, KVH, HD)
-    past_values = cache_values.reshape(local_rows, cache_span, KVH, HD)
-    score_scale = 1.0 / math.sqrt(HD)
-    past_scores = (
-        jnp.einsum("tgqd,tcgd->tgqc", query_heads, past_keys, preferred_element_type=jnp.float32)
-        * score_scale
-    )
-    own_scores = (
-        jnp.einsum(
-            "tgqd,tgd->tgq",
-            query_heads,
-            new_keys.reshape(local_rows, KVH, HD),
-            preferred_element_type=jnp.float32,
-        )
-        * score_scale
-    )
-    is_valid = lax.broadcasted_iota(jnp.int32, (local_rows, cache_span), 1) < cache_len[:, None]
-    past_scores = jnp.where(is_valid[:, None, None, :], past_scores, -1e30)
-    peak_score = jnp.maximum(jnp.max(past_scores, axis=3), own_scores)
-    past_exp = jnp.exp(past_scores - peak_score[..., None])
-    own_exp = jnp.exp(own_scores - peak_score)
-    denom_sum = jnp.sum(past_exp, axis=3) + own_exp
-    past_weights = (past_exp / denom_sum[..., None]).astype(jnp.bfloat16)
-    own_weights = (own_exp / denom_sum).astype(jnp.bfloat16)
-    blended = jnp.einsum(
-        "tgqc,tcgd->tgqd", past_weights, past_values, preferred_element_type=jnp.float32
-    )
-    blended = blended + own_weights.astype(jnp.float32)[..., None] * new_values.reshape(
-        local_rows, KVH, 1, HD
-    ).astype(jnp.float32)
-    return blended.reshape(local_rows, H * HD).astype(jnp.bfloat16)
+def attend(lengths, keys, values, q32, own_keys, own_values, blended32, arrived):
+    group = H // KVH
+    scale = 1.0 / math.sqrt(HD)
+
+    def token(t):
+        position = lax.broadcasted_iota(jnp.int32, (group, keys.shape[1]), 1)
+        kept = position < lengths[t]
+        for g in range(KVH):
+            cols = slice(g * HD, (g + 1) * HD)
+            heads = pl.ds(g * group * 16 + t, group, stride=16)
+            q = q32[heads, :]
+            scores = lax.dot_general(
+                q.astype(jnp.bfloat16), keys[t, :, cols], (((1,), (1,)), ((), ())),
+                preferred_element_type=jnp.float32,
+            )
+            scores = jnp.where(kept, scores * scale, -1e30)
+            own = jnp.sum(q * own_keys[pl.ds(t, 1), cols], axis=1, keepdims=True) * scale
+            peak = jnp.maximum(jnp.max(scores, axis=1, keepdims=True), own)
+            grown, own_grown = jnp.exp(scores - peak), jnp.exp(own - peak)
+            total = jnp.sum(grown, axis=1, keepdims=True) + own_grown
+            weights = (grown / total).astype(jnp.bfloat16)
+            own_weight = (own_grown / total).astype(jnp.bfloat16).astype(jnp.float32)
+            mixed = jnp.dot(weights, values[t, :, cols], preferred_element_type=jnp.float32)
+            blended32[heads, :] = mixed + own_weight * own_values[pl.ds(t, 1), cols]
+
+    for chunk in range(4):
+        arrived(chunk)
+
+        @pl.loop(4 * chunk, 4 * chunk + 4, unroll=4)
+        def _(t):
+            token(t)
 
 
 class Place:
@@ -525,7 +520,8 @@
 
 
 def project_kernel(
-    att, resid_hbm, gain_hbm, router_hbm, ids_hbm, w_hbm, hidden_out, x_out,
+    lengths, q_hbm, nk_hbm, nv_hbm, key_hbm, value_hbm, resid_hbm, gain_hbm, router_hbm, ids_hbm, w_hbm, hidden_out, x_out,
+    q, nk, nv, keys, values, q32, own_keys, own_values, blended32, att,
     resid, gain, router, ids, w, seen, part, pair_out, pair_in, ra1, ra2, rc,
     send_sem, recv_sem, all_send, all_recv, load_sem,
 ):
@@ -542,7 +538,16 @@
             ((w_hbm, w), (resid_hbm, resid), (gain_hbm, gain), (router_hbm, router), (ids_hbm, ids))
         )
     ]
-    for copy in loads:
+    heads = [
+        pltpu.make_async_copy(src, dst, load_sem.at[5 + i])
+        for i, (src, dst) in enumerate(((q_hbm, q), (nk_hbm, nk), (nv_hbm, nv)))
+    ]
+    cached = [
+        pltpu.make_async_copy(src.at[pl.ds(4 * i, 4)], dst.at[pl.ds(4 * i, 4)], load_sem.at[8 + 2 * i + n])
+        for i in range(4)
+        for n, (src, dst) in enumerate(((key_hbm, keys), (value_hbm, values)))
+    ]
+    for copy in heads + cached + loads:
         copy.start()
 
     def send(src, dst, key, dev):
@@ -569,13 +574,26 @@
     barrier = pltpu.get_barrier_semaphore()
     for k in range(1, 32):
         pl.semaphore_signal(barrier, inc=1, device_id=(lax.rem(ep + k, 32), dp), device_id_type=MESH)
-    seen[slot(ep)] = att[:, pl.ds(pl.multiple_of(ep * 256, 256), 256)]
+    for copy in heads:
+        copy.wait()
+    for h in range(H):
+        q32[h * 16 : (h + 1) * 16, :] = q[:, h * HD : (h + 1) * HD].astype(jnp.float32)
+    own_keys[...] = nk[...].astype(jnp.float32)
+    own_values[...] = nv[...].astype(jnp.float32)
+
+    def arrived(chunk):
+        cached[2 * chunk].wait()
+        cached[2 * chunk + 1].wait()
+
+    attend(lengths, keys, values, q32, own_keys, own_values, blended32, arrived)
+    att[...] = blended32[...].astype(jnp.bfloat16).reshape(H, 16, HD)
+    seen[slot(ep)] = att[pl.ds(2 * ep, 2)]
     pl.semaphore_wait(barrier, 31)
 
     for k in range(1, 32):
         to = lax.rem(ep + k, 32)
         pltpu.make_async_remote_copy(
-            src_ref=att.at[:, pl.ds(pl.multiple_of(to * 256, 256), 256)],
+            src_ref=att.at[pl.ds(2 * to, 2)],
             dst_ref=seen.at[slot(ep)],
             send_sem=all_send.at[0],
             recv_sem=all_recv.at[0],
@@ -601,9 +619,11 @@
         @pl.loop(0, HALF // 256, unroll=4)
         def _(n):
             start = pl.multiple_of(n * 256, 256)
-            theirs = seen[pl.ds(other * 16, 16)].reshape(256, 256)
-            ours = seen[pl.ds(c * 16, 16)].reshape(256, 256)
-            rows = jnp.concatenate([theirs, ours], axis=0)
+            halves = [
+                jnp.concatenate([seen[pl.ds(core * 16, 16), i].reshape(256, HD) for core in (other, c)], axis=0)
+                for i in range(2)
+            ]
+            rows = jnp.concatenate(halves, axis=1)
             cols = pl.ds(pl.multiple_of(q * HALF + start, 256), 256)
             y = jnp.dot(rows, w[:, cols], preferred_element_type=jnp.float32).astype(jnp.bfloat16)
             pair_out[q, :, :, :, pl.ds(start, 256)] = y[:256].reshape(4, 4, 16, 256)
@@ -707,7 +727,9 @@
     assert len(names.table) == 26
 
 
-def attention_out(attended, resid, norm_gain, router, expert_ids, out_proj):
+def attention_out(
+    cache_len, queries, new_keys, new_values, cache_keys, cache_values, resid, norm_gain, router, expert_ids, out_proj
+):
     bf = jnp.bfloat16
     vmem = pl.BlockSpec(memory_space=pltpu.VMEM)
     return pl.pallas_call(
@@ -716,15 +738,25 @@
             jax.ShapeDtypeStruct((16, D), jnp.float32),
             jax.ShapeDtypeStruct((16, 3 * PART), bf),
         ),
-        in_specs=[vmem] + [pl.BlockSpec(memory_space=pl.ANY)] * 5,
+        in_specs=[pl.BlockSpec(memory_space=pltpu.SMEM)] + [pl.BlockSpec(memory_space=pl.ANY)] * 10,
         out_specs=(vmem, vmem),
         scratch_shapes=[
+            pltpu.VMEM(queries.shape, bf),
+            pltpu.VMEM(new_keys.shape, bf),
+            pltpu.VMEM(new_values.shape, bf),
+            pltpu.VMEM(cache_keys.shape, bf),
+            pltpu.VMEM(cache_values.shape, bf),
+            pltpu.VMEM((16 * H, HD), jnp.float32),
+            pltpu.VMEM(new_keys.shape, jnp.float32),
+            pltpu.VMEM(new_values.shape, jnp.float32),
+            pltpu.VMEM((16 * H, HD), jnp.float32),
+            pltpu.VMEM((H, 16, HD), bf),
             pltpu.VMEM((16, D), bf),
             pltpu.VMEM((1, D), jnp.float32),
             pltpu.VMEM(router.shape[::-1], bf),
             pltpu.VMEM((TOP, 16), jnp.int32),
             pltpu.VMEM((256, D), bf),
-            pltpu.VMEM((32, 16, 256), bf),
+            pltpu.VMEM((32, 2, 16, HD), bf),
             pltpu.VMEM((2, 4, 4, 16, HALF), bf),
             pltpu.VMEM((2, 4, 4, 16, HALF), bf),
             pltpu.VMEM((2, 4, 4, 16, HALF), bf),
@@ -735,13 +767,13 @@
             pltpu.SemaphoreType.DMA((26,)),
             pltpu.SemaphoreType.DMA((1,)),
             pltpu.SemaphoreType.DMA((1,)),
-            pltpu.SemaphoreType.DMA((5,)),
+            pltpu.SemaphoreType.DMA((16,)),
         ],
         compiler_params=pltpu.CompilerParams(
             collective_id=1, has_side_effects=True, vmem_limit_bytes=67043328
         ),
         name="attention_out",
-    )(attended, resid, norm_gain.reshape(1, D), router.T, expert_ids.T, out_proj)
+    )(cache_len, queries, new_keys, new_values, cache_keys, cache_values, resid, norm_gain.reshape(1, D), router.T, expert_ids.T, out_proj)
 
 
 def local(
@@ -760,8 +792,9 @@
     up_slab,
     down_slab,
 ):
-    attended = attend(queries, new_keys, new_values, cache_keys, cache_values, cache_len)
-    hidden, x_in = attention_out(attended, resid, norm_gain, router, expert_ids, out_proj)
+    hidden, x_in = attention_out(
+        cache_len, queries, new_keys, new_values, cache_keys, cache_values, resid, norm_gain, router, expert_ids, out_proj
+    )
     return moe(x_in, hidden, gate_slab[0], up_slab[0], down_slab[0])
 
 

time: 143 us -> 153 us (1.070)
  Pallas kernels: 132 us -> 151 us
  matrix products: 4.03 us -> 0 us
  local copies, waits for them, and re-layouts: 5.02 us -> 1.67 us
    pallas_call x1, Pallas kernels: 33.2 us -> 51 us  [attention_out(): pl.pallas_call(project_kernel, out_shape=(jax.ShapeDtypeStruct((16, D), j...]
    dot_general x3 -> x0, matrix products: 4.03 us -> none  [the longest x1 3.03 us: attend(): jnp.einsum('tgqd,tcgd->tgqc', query_heads, past_keys, preferred_element_t...]
    unnamed x5 -> x1, local copies, waits for them, and re-layouts: 3.55 us -> 1.67 us
where the time goes in v5:
time: 153 us
  Pallas kernels  151 us (99%)
  local copies, waits for them, and re-layouts  1.67 us (1%)
    pallas_call x1, Pallas kernels, moe(): pl.pallas_call(moe_kernel, out_shape=jax.ShapeDtypeStruct((16, D), jnp.fl...  100 us
    pallas_call x1, Pallas kernels, attention_out(): pl.pallas_call(project_kernel, out_shape=(jax.ShapeDtypeStruct((16, D), j...  51 us

profile of v5, /device:TPU:1, one launch (start us, length us, event | category | flops | bytes accessed | tf_op | source)
XLA Modules:
  0.0 152.8 jit_solution(833313042056191650)
XLA Ops:
  0.0 51.0 %attention_out.1 = (f32[16,4096]{1,0:T(8,128)}, bf16[16,4224]{1,0:T(8,128)(2,1)}) custom-call(s32[16]{0:T(128)} %lengths.1, bf16[16,8192]{1,0:T(8,128)(2,1)} %q_hbm.1, bf16[16,512]{1,0:T(8,128)(2,1)} %nk_hbm.1, bf16[16,512]{1,0:T(8,128)(2,1)} %nv_hbm.1, bf16[16,128,512]{2,1,0:T(8,128)(2,1)} %key_hbm.1, bf16[16,128,512]{2,1,0:T(8,128)(2,1)} %value_hbm.1, ...), custom_call_target="tpu_custom_call" | custom-call | tf_op jit(solution)/shard_map/attention_out/pallas_call | solution.py:735
  51.0 100.1 %moe.1 = f32[16,4096]{1,0:T(8,128)} custom-call(bf16[16,4224]{1,0:T(8,128)(2,1)} %get-tuple-element.7.x_in, f32[16,4096]{1,0:T(8,128)} %get-tuple-element.8.hidden, bf16[4096,384]{1,0:T(8,128)(2,1)} %bitcast.6, bf16[4096,384]{1,0:T(8,128)(2,1)} %bitcast.7, bf16[384,4096]{1,0:T(8,128)(2,1)} %bitcast.8), custom_call_target="tpu_custom_call" | custom-call | tf_op jit(solution)/shard_map/moe/pallas_call | solution.py:488
  151.1 1.7 %copy.16 = f32[16,4096]{1,0:T(8,128)} copy(f32[16,4096]{1,0:T(8,128)} %moe.1) | data formatting | bytes 524288

commit v6 on v5

--- a/solution.py
+++ b/solution.py
@@ -25,25 +25,33 @@
     scale = 1.0 / math.sqrt(HD)
 
     def token(t):
-        position = lax.broadcasted_iota(jnp.int32, (group, keys.shape[1]), 1)
+        position = lax.broadcasted_iota(jnp.int32, (group * KVH, keys.shape[1]), 1)
         kept = position < lengths[t]
-        for g in range(KVH):
-            cols = slice(g * HD, (g + 1) * HD)
-            heads = pl.ds(g * group * 16 + t, group, stride=16)
-            q = q32[heads, :]
-            scores = lax.dot_general(
-                q.astype(jnp.bfloat16), keys[t, :, cols], (((1,), (1,)), ((), ())),
-                preferred_element_type=jnp.float32,
-            )
-            scores = jnp.where(kept, scores * scale, -1e30)
-            own = jnp.sum(q * own_keys[pl.ds(t, 1), cols], axis=1, keepdims=True) * scale
-            peak = jnp.maximum(jnp.max(scores, axis=1, keepdims=True), own)
-            grown, own_grown = jnp.exp(scores - peak), jnp.exp(own - peak)
-            total = jnp.sum(grown, axis=1, keepdims=True) + own_grown
-            weights = (grown / total).astype(jnp.bfloat16)
-            own_weight = (own_grown / total).astype(jnp.bfloat16).astype(jnp.float32)
-            mixed = jnp.dot(weights, values[t, :, cols], preferred_element_type=jnp.float32)
-            blended32[heads, :] = mixed + own_weight * own_values[pl.ds(t, 1), cols]
+        slices = [slice(g * HD, (g + 1) * HD) for g in range(KVH)]
+        qs = [q32[pl.ds(g * group * 16 + t, group, stride=16), :] for g in range(KVH)]
+        scores = jnp.concatenate(
+            [
+                lax.dot_general(
+                    q.astype(jnp.bfloat16), keys[t, :, cols], (((1,), (1,)), ((), ())),
+                    preferred_element_type=jnp.float32,
+                )
+                for q, cols in zip(qs, slices)
+            ],
+            axis=0,
+        )
+        scores = jnp.where(kept, scores * scale, -1e30)
+        own = jnp.concatenate([q * own_keys[pl.ds(t, 1), cols] for q, cols in zip(qs, slices)], axis=0)
+        own = jnp.sum(own, axis=1, keepdims=True) * scale
+        peak = jnp.maximum(jnp.max(scores, axis=1, keepdims=True), own)
+        grown, own_grown = jnp.exp(scores - peak), jnp.exp(own - peak)
+        total = jnp.sum(grown, axis=1, keepdims=True) + own_grown
+        weights = (grown / total).astype(jnp.bfloat16)
+        own_weight = (own_grown / total).astype(jnp.bfloat16).astype(jnp.float32)
+        for g, cols in enumerate(slices):
+            here = slice(g * group, (g + 1) * group)
+            mixed = jnp.dot(weights[here], values[t, :, cols], preferred_element_type=jnp.float32)
+            mixed += own_weight[here] * own_values[pl.ds(t, 1), cols]
+            blended32[pl.ds(g * group * 16 + t, group, stride=16), :] = mixed
 
     for chunk in range(4):
         arrived(chunk)

time: 153 us -> 138 us (0.902)
  Pallas kernels: 151 us -> 136 us
    pallas_call x1, Pallas kernels: 51 us -> 36.3 us  [attention_out(): pl.pallas_call(project_kernel, out_shape=(jax.ShapeDtypeStruct((16, D), j...]
where the time goes in v6:
time: 138 us
  Pallas kernels  136 us (99%)
  local copies, waits for them, and re-layouts  1.67 us (1%)
    pallas_call x1, Pallas kernels, moe(): pl.pallas_call(moe_kernel, out_shape=jax.ShapeDtypeStruct((16, D), jnp.fl...  99.9 us
    pallas_call x1, Pallas kernels, attention_out(): pl.pallas_call(project_kernel, out_shape=(jax.ShapeDtypeStruct((16, D), j...  36.3 us

profile of v6, /device:TPU:1, one launch (start us, length us, event | category | flops | bytes accessed | tf_op | source)
XLA Modules:
  0.0 138.0 jit_solution(18226979736476826758)
XLA Ops:
  0.0 36.3 %attention_out.1 = (f32[16,4096]{1,0:T(8,128)}, bf16[16,4224]{1,0:T(8,128)(2,1)}) custom-call(s32[16]{0:T(128)} %lengths.1, bf16[16,8192]{1,0:T(8,128)(2,1)} %q_hbm.1, bf16[16,512]{1,0:T(8,128)(2,1)} %nk_hbm.1, bf16[16,512]{1,0:T(8,128)(2,1)} %nv_hbm.1, bf16[16,128,512]{2,1,0:T(8,128)(2,1)} %key_hbm.1, bf16[16,128,512]{2,1,0:T(8,128)(2,1)} %value_hbm.1, ...), custom_call_target="tpu_custom_call" | custom-call | tf_op jit(solution)/shard_map/attention_out/pallas_call | solution.py:743
  36.4 99.9 %moe.1 = f32[16,4096]{1,0:T(8,128)} custom-call(bf16[16,4224]{1,0:T(8,128)(2,1)} %get-tuple-element.7.x_in, f32[16,4096]{1,0:T(8,128)} %get-tuple-element.8.hidden, bf16[4096,384]{1,0:T(8,128)(2,1)} %bitcast.6, bf16[4096,384]{1,0:T(8,128)(2,1)} %bitcast.7, bf16[384,4096]{1,0:T(8,128)(2,1)} %bitcast.8), custom_call_target="tpu_custom_call" | custom-call | tf_op jit(solution)/shard_map/moe/pallas_call | solution.py:496
  136.3 1.7 %copy.16 = f32[16,4096]{1,0:T(8,128)} copy(f32[16,4096]{1,0:T(8,128)} %moe.1) | data formatting | bytes 524288

commit v7 on v6

--- a/solution.py
+++ b/solution.py
@@ -307,7 +307,7 @@
     def activate_opposite(p):
         far = rel(dims[p][2], 2)
 
-        @pl.loop(0, 8)
+        @pl.loop(0, 8, unroll=2)
         def _(i):
             core, k = i // 4, lax.rem(i, 4)
             activate(((core, k, every, far), (core, k, far, every), (core, far, k, every))[p])
@@ -354,12 +354,10 @@
             part[p, o1, :, :, :, 1280:] = jnp.zeros((4, 4, 16, 128), jnp.bfloat16)
 
     def add(dst, *srcs):
-        @pl.loop(0, 4)
-        def _(i):
-            total = dst[i].astype(jnp.float32)
-            for s in srcs:
-                total += s[i].astype(jnp.float32)
-            dst[i] = total.astype(jnp.bfloat16)
+        total = dst[...].astype(jnp.float32)
+        for s in srcs:
+            total += s[...].astype(jnp.float32)
+        dst[...] = total.astype(jnp.bfloat16)
 
     def add_sub(dst, *srcs):
         total = dst[...].astype(jnp.float32)
@@ -375,7 +373,8 @@
 
             @pl.loop(0, 4)
             def _(i):
-                add(part.at[p, o1, i], pair_in.at[p, o1, i])
+                total = part[p, o1, i].astype(jnp.float32) + pair_in[p, o1, i].astype(jnp.float32)
+                part[p, o1, i] = total.astype(jnp.bfloat16)
 
             then(p)
 

time: 138 us -> 137 us (level)
  no operation moved by 1% of the time
where the time goes in v7:
time: 137 us
  Pallas kernels  136 us (99%)
  local copies, waits for them, and re-layouts  1.67 us (1%)
    pallas_call x1, Pallas kernels, moe(): pl.pallas_call(moe_kernel, out_shape=jax.ShapeDtypeStruct((16, D), jnp.fl...  99.2 us
    pallas_call x1, Pallas kernels, attention_out(): pl.pallas_call(project_kernel, out_shape=(jax.ShapeDtypeStruct((16, D), j...  36.3 us

profile of v7, /device:TPU:1, one launch (start us, length us, event | category | flops | bytes accessed | tf_op | source)
XLA Modules:
  0.0 137.3 jit_solution(12912628124779049275)
XLA Ops:
  0.0 36.3 %attention_out.1 = (f32[16,4096]{1,0:T(8,128)}, bf16[16,4224]{1,0:T(8,128)(2,1)}) custom-call(s32[16]{0:T(128)} %lengths.1, bf16[16,8192]{1,0:T(8,128)(2,1)} %q_hbm.1, bf16[16,512]{1,0:T(8,128)(2,1)} %nk_hbm.1, bf16[16,512]{1,0:T(8,128)(2,1)} %nv_hbm.1, bf16[16,128,512]{2,1,0:T(8,128)(2,1)} %key_hbm.1, bf16[16,128,512]{2,1,0:T(8,128)(2,1)} %value_hbm.1, ...), custom_call_target="tpu_custom_call" | custom-call | tf_op jit(solution)/shard_map/attention_out/pallas_call | solution.py:742
  36.4 99.2 %moe.1 = f32[16,4096]{1,0:T(8,128)} custom-call(bf16[16,4224]{1,0:T(8,128)(2,1)} %get-tuple-element.7.x_in, f32[16,4096]{1,0:T(8,128)} %get-tuple-element.8.hidden, bf16[4096,384]{1,0:T(8,128)(2,1)} %bitcast.6, bf16[4096,384]{1,0:T(8,128)(2,1)} %bitcast.7, bf16[384,4096]{1,0:T(8,128)(2,1)} %bitcast.8), custom_call_target="tpu_custom_call" | custom-call | tf_op jit(solution)/shard_map/moe/pallas_call | solution.py:495
  135.6 1.7 %copy.16 = f32[16,4096]{1,0:T(8,128)} copy(f32[16,4096]{1,0:T(8,128)} %moe.1) | data formatting | bytes 524288
